TPU v7x, 32 devices: a whole 2x2x4 slice. The times are simulated.
32 devices in a mesh: blk: 16 (over z, y, core), rows: 2 (over x).
Axes of the slice: x: 2, y: 2, z: 4, core: 2. Of those that a mesh axis runs over, the one named last changes fastest.
Arguments:
- columns: float32 [2048, 1280], P('blk', 'rows'), may hold values from -9 to 9
- right_factor: float32 [2048, 512], P('blk', 'rows'), may hold values from -6 to 6
Outputs:
- new_columns: float32 [2048, 1280], P('blk', 'rows')
- new_factor: float32 [2048, 512], P('blk', 'rows')
All inputs are finite; a program needn't handle non-finite values.
Results may differ from a plain program's by a relative error of at most 0.0003.
Values sent between devices are 32-bit elements; how exact they have to be, the bound alone decides.
No kernel may reach another device: no remote copies, remote signals or barrier semaphores. Data moves between devices by JAX's collectives and lax.ppermute only.
A program may use at most 64 MiB of HBM per device.

v0:
```python
import jax
import jax.numpy as jnp
from jax import lax
from jax.sharding import PartitionSpec as P

STEPS = 6


HIGHEST_PREC = lax.Precision.HIGHEST


def shifted(block, axis, distance):
    devices = range(lax.axis_size(axis))
    route = [((i - distance) % len(devices), i) for i in devices]
    return lax.ppermute(block, axis, route)


def orth_factor(square):
    lower_factor = jnp.linalg.cholesky(jnp.dot(square.T, square, precision=HIGHEST_PREC))
    return jax.scipy.linalg.solve_triangular(lower_factor, square.T, lower=True).T


def rotation(pair_gram):
    first_turn = orth_factor(pair_gram)
    return orth_factor(jnp.dot(pair_gram, first_turn, precision=HIGHEST_PREC))


def gram_of(upper_rows, lower_rows):
    return lax.dot_general(upper_rows, lower_rows, (((1,), (1,)), ((), ())), precision=HIGHEST_PREC)


def rotate(rotation_matrix, blocks):
    return lax.dot_general(
        rotation_matrix, blocks, (((0,), (0,)), ((), ())), precision=HIGHEST_PREC
    )


def body(columns, right_factor):
    block_width = columns.shape[0] // 2
    stay_gram, moving_gram = lax.psum(
        (
            gram_of(columns[:block_width], columns[:block_width]),
            gram_of(columns[block_width:], columns[block_width:]),
        ),
        "rows",
    )

    def advance_cross(step_index, loop_state):
        column_pair, factor_pair, stay_gram, moving_gram = loop_state
        cross_term = lax.psum(gram_of(column_pair[:block_width], column_pair[block_width:]), "rows")
        upper_half = jnp.concatenate([stay_gram, cross_term], 1)
        lower_half = jnp.concatenate([cross_term.T, moving_gram], 1)
        pair_gram = jnp.concatenate([upper_half, lower_half], 0)
        rotation_matrix = rotation(pair_gram)
        column_pair = rotate(rotation_matrix, column_pair)
        factor_pair = rotate(rotation_matrix, factor_pair)
        rotated_gram = rotate(
            rotation_matrix, jnp.dot(pair_gram, rotation_matrix, precision=HIGHEST_PREC)
        )
        arrived = shifted(
            (
                column_pair[block_width:],
                factor_pair[block_width:],
                rotated_gram[block_width:, block_width:],
            ),
            "blk",
            1,
        )
        return (
            jnp.concatenate([column_pair[:block_width], arrived[0]], 0),
            jnp.concatenate([factor_pair[:block_width], arrived[1]], 0),
            rotated_gram[:block_width, :block_width],
            arrived[2],
        )

    result = lax.fori_loop(0, STEPS, advance_cross, (columns, right_factor, stay_gram, moving_gram))
    return (result[0], result[1])


def solution(mesh):
    return jax.shard_map(
        body,
        mesh=mesh,
        in_specs=(P("blk", "rows"), P("blk", "rows")),
        out_specs=(P("blk", "rows"), P("blk", "rows")),
        check_vma=False,
    )
```

profile of v0, /device:TPU:0, one launch (start us, length us, event | category | flops | bytes accessed | tf_op | source)
XLA Modules:
  0.0 402.2 jit_solution(8088612820644958071)
XLA Ops:
  2.2 10.4 %all-reduce = (f32[64,64]{1,0:T(8,128)S(1)}, f32[64,64]{1,0:T(8,128)S(1)}) all-reduce(f32[64,64]{1,0:T(8,128)S(1)} %fusion.17, f32[64,64]{1,0:T(8,128)S(1)} %fusion.15), channel_id=1, replica_groups=mesh['blk'=16,'rows'=2] {'rows'}, use_global_device_ids=true, to_apply=%region_0.0 | all-reduce | flops 8192 | bytes 65536 | tf_op jit(solution)/shard_map/psum | solution.py:40
  12.7 388.7 %while.16 = (s32[]{:T(128)}, f32[128,640]{1,0:T(8,128)S(1)}, f32[128,256]{1,0:T(8,128)S(1)}, f32[64,64]{1,0:T(8,128)S(1)}, f32[64,64]{1,0:T(8,128)S(1)}, /*index=5*/s32[]{:T(128)}) while((s32[]{:T(128)}, f32[128,640]{1,0:T(8,128)S(1)}, f32[128,256]{1,0:T(8,128)S(1)}, f32[64,64]{1,0:T(8,128)S(1)}, f32[64,64]{1,0:T(8,128)S(1)}, ...), condition=%wide.region_6.9_spmd, body=%wide.region_2.8_spmd.sunk | while | flops 384241920 | bytes 6834369 | solution.py:76
  20.7 11.7 %cholesky.144 = f32[128,128]{1,0:T(8,128)S(1)} custom-call(f32[128,128]{1,0:T(8,128)S(1)} %fusion.103), custom_call_target="Cholesky" | custom-call | tf_op jit(solution)/shard_map/while/body/eval_jaxpr/jit(cholesky)/cholesky | solution.py:19
  33.7 9.8 %custom-call.10 = f32[1,128,128]{1,2,0:T(8,128)S(1)} custom-call(f32[1,128,128]{2,1,0:T(8,128)S(1)} %fusion.105), custom_call_target="InvertDiagBlocksLowerTriangular" | custom-call | tf_op jit(solution)/shard_map/while/body/eval_jaxpr/jit(_solve_triangular)/triangular_solve | solution.py:20
  44.5 11.7 %cholesky.145 = f32[128,128]{1,0:T(8,128)S(1)} custom-call(f32[128,128]{1,0:T(8,128)S(1)} %fusion.109), custom_call_target="Cholesky" | custom-call | tf_op jit(solution)/shard_map/while/body/eval_jaxpr/jit(cholesky)/cholesky | solution.py:19
  57.6 9.8 %custom-call.11 = f32[1,128,128]{1,2,0:T(8,128)S(1)} custom-call(f32[1,128,128]{2,1,0:T(8,128)S(1)} %fusion.110), custom_call_target="InvertDiagBlocksLowerTriangular" | custom-call | tf_op jit(solution)/shard_map/while/body/eval_jaxpr/jit(_solve_triangular)/triangular_solve | solution.py:20
  86.5 11.7 %cholesky.144 = f32[128,128]{1,0:T(8,128)S(1)} custom-call(f32[128,128]{1,0:T(8,128)S(1)} %fusion.103), custom_call_target="Cholesky" | custom-call | tf_op jit(solution)/shard_map/while/body/eval_jaxpr/jit(cholesky)/cholesky | solution.py:19
  99.5 9.8 %custom-call.10 = f32[1,128,128]{1,2,0:T(8,128)S(1)} custom-call(f32[1,128,128]{2,1,0:T(8,128)S(1)} %fusion.105), custom_call_target="InvertDiagBlocksLowerTriangular" | custom-call | tf_op jit(solution)/shard_map/while/body/eval_jaxpr/jit(_solve_triangular)/triangular_solve | solution.py:20
  110.4 11.7 %cholesky.145 = f32[128,128]{1,0:T(8,128)S(1)} custom-call(f32[128,128]{1,0:T(8,128)S(1)} %fusion.109), custom_call_target="Cholesky" | custom-call | tf_op jit(solution)/shard_map/while/body/eval_jaxpr/jit(cholesky)/cholesky | solution.py:19
  123.4 9.8 %custom-call.11 = f32[1,128,128]{1,2,0:T(8,128)S(1)} custom-call(f32[1,128,128]{2,1,0:T(8,128)S(1)} %fusion.110), custom_call_target="InvertDiagBlocksLowerTriangular" | custom-call | tf_op jit(solution)/shard_map/while/body/eval_jaxpr/jit(_solve_triangular)/triangular_solve | solution.py:20
  150.8 11.7 %cholesky.144 = f32[128,128]{1,0:T(8,128)S(1)} custom-call(f32[128,128]{1,0:T(8,128)S(1)} %fusion.103), custom_call_target="Cholesky" | custom-call | tf_op jit(solution)/shard_map/while/body/eval_jaxpr/jit(cholesky)/cholesky | solution.py:19
  163.8 9.8 %custom-call.10 = f32[1,128,128]{1,2,0:T(8,128)S(1)} custom-call(f32[1,128,128]{2,1,0:T(8,128)S(1)} %fusion.105), custom_call_target="InvertDiagBlocksLowerTriangular" | custom-call | tf_op jit(solution)/shard_map/while/body/eval_jaxpr/jit(_solve_triangular)/triangular_solve | solution.py:20
  174.6 11.7 %cholesky.145 = f32[128,128]{1,0:T(8,128)S(1)} custom-call(f32[128,128]{1,0:T(8,128)S(1)} %fusion.109), custom_call_target="Cholesky" | custom-call | tf_op jit(solution)/shard_map/while/body/eval_jaxpr/jit(cholesky)/cholesky | solution.py:19
  187.7 9.8 %custom-call.11 = f32[1,128,128]{1,2,0:T(8,128)S(1)} custom-call(f32[1,128,128]{2,1,0:T(8,128)S(1)} %fusion.110), custom_call_target="InvertDiagBlocksLowerTriangular" | custom-call | tf_op jit(solution)/shard_map/while/body/eval_jaxpr/jit(_solve_triangular)/triangular_solve | solution.py:20
  216.0 11.7 %cholesky.144 = f32[128,128]{1,0:T(8,128)S(1)} custom-call(f32[128,128]{1,0:T(8,128)S(1)} %fusion.103), custom_call_target="Cholesky" | custom-call | tf_op jit(solution)/shard_map/while/body/eval_jaxpr/jit(cholesky)/cholesky | solution.py:19
  229.1 9.8 %custom-call.10 = f32[1,128,128]{1,2,0:T(8,128)S(1)} custom-call(f32[1,128,128]{2,1,0:T(8,128)S(1)} %fusion.105), custom_call_target="InvertDiagBlocksLowerTriangular" | custom-call | tf_op jit(solution)/shard_map/while/body/eval_jaxpr/jit(_solve_triangular)/triangular_solve | solution.py:20
  239.9 11.7 %cholesky.145 = f32[128,128]{1,0:T(8,128)S(1)} custom-call(f32[128,128]{1,0:T(8,128)S(1)} %fusion.109), custom_call_target="Cholesky" | custom-call | tf_op jit(solution)/shard_map/while/body/eval_jaxpr/jit(cholesky)/cholesky | solution.py:19
  252.9 9.8 %custom-call.11 = f32[1,128,128]{1,2,0:T(8,128)S(1)} custom-call(f32[1,128,128]{2,1,0:T(8,128)S(1)} %fusion.110), custom_call_target="InvertDiagBlocksLowerTriangular" | custom-call | tf_op jit(solution)/shard_map/while/body/eval_jaxpr/jit(_solve_triangular)/triangular_solve | solution.py:20
  280.3 11.7 %cholesky.144 = f32[128,128]{1,0:T(8,128)S(1)} custom-call(f32[128,128]{1,0:T(8,128)S(1)} %fusion.103), custom_call_target="Cholesky" | custom-call | tf_op jit(solution)/shard_map/while/body/eval_jaxpr/jit(cholesky)/cholesky | solution.py:19
  293.4 9.8 %custom-call.10 = f32[1,128,128]{1,2,0:T(8,128)S(1)} custom-call(f32[1,128,128]{2,1,0:T(8,128)S(1)} %fusion.105), custom_call_target="InvertDiagBlocksLowerTriangular" | custom-call | tf_op jit(solution)/shard_map/while/body/eval_jaxpr/jit(_solve_triangular)/triangular_solve | solution.py:20
  304.2 11.7 %cholesky.145 = f32[128,128]{1,0:T(8,128)S(1)} custom-call(f32[128,128]{1,0:T(8,128)S(1)} %fusion.109), custom_call_target="Cholesky" | custom-call | tf_op jit(solution)/shard_map/while/body/eval_jaxpr/jit(cholesky)/cholesky | solution.py:19
  345.5 11.7 %cholesky.144 = f32[128,128]{1,0:T(8,128)S(1)} custom-call(f32[128,128]{1,0:T(8,128)S(1)} %fusion.103), custom_call_target="Cholesky" | custom-call | tf_op jit(solution)/shard_map/while/body/eval_jaxpr/jit(cholesky)/cholesky | solution.py:19
  358.6 9.8 %custom-call.10 = f32[1,128,128]{1,2,0:T(8,128)S(1)} custom-call(f32[1,128,128]{2,1,0:T(8,128)S(1)} %fusion.105), custom_call_target="InvertDiagBlocksLowerTriangular" | custom-call | tf_op jit(solution)/shard_map/while/body/eval_jaxpr/jit(_solve_triangular)/triangular_solve | solution.py:20
  369.4 11.7 %cholesky.145 = f32[128,128]{1,0:T(8,128)S(1)} custom-call(f32[128,128]{1,0:T(8,128)S(1)} %fusion.109), custom_call_target="Cholesky" | custom-call | tf_op jit(solution)/shard_map/while/body/eval_jaxpr/jit(cholesky)/cholesky | solution.py:19
  (227 shorter events, 151.3 us)
Async XLA Ops:
  1.9 10.8 %copy-start.2 = (f32[128,256]{1,0:T(8,128)S(1)}, f32[128,256]{1,0:T(8,128)}, u32[]{:S(2)}) copy-start(f32[128,256]{1,0:T(8,128)} %param.8) | copy-start | bytes 393220
  68.0 6.4 %collective-permute-start.1 = (f32[64,256]{1,0:T(8,128)S(1)}, f32[64,256]{1,0:T(8,128)S(1)}, u32[]{:S(2)}, u32[]{:S(2)}) collective-permute-start(f32[64,256]{1,0:T(8,128)S(1)} %get-tuple-element.91), channel_id=1, source_target_pairs={{30,0},{0,2},{2,4},{4,6},{6,8},{8,10},{10,12},{12,14},{14,16},{16,... | collective-permute-start | bytes 196616 | tf_op jit(solution)/shard_map/while/body/eval_jaxpr/ppermute | solution.py:15
  68.5 7.7 %collective-permute-start = (f32[64,640]{1,0:T(8,128)S(1)}, f32[64,640]{1,0:T(8,128)S(1)}, u32[]{:S(2)}, u32[]{:S(2)}) collective-permute-start(f32[64,640]{1,0:T(8,128)S(1)} %get-tuple-element.89), channel_id=1, source_target_pairs={{30,0},{0,2},{2,4},{4,6},{6,8},{8,10},{10,12},{12,14},{14,16},{16,... | collective-permute-start | bytes 491528 | tf_op jit(solution)/shard_map/while/body/eval_jaxpr/ppermute | solution.py:15
  71.1 6.0 %collective-permute-start.2 = (f32[64,64]{1,0:T(8,128)S(1)}, f32[64,64]{1,0:T(8,128)S(1)}, u32[]{:S(2)}, u32[]{:S(2)}) collective-permute-start(f32[64,64]{1,0:T(8,128)S(1)} %get-tuple-element.94), channel_id=1, source_target_pairs={{30,0},{0,2},{2,4},{4,6},{6,8},{8,10},{10,12},{12,14},{14,16},{16,... | collective-permute-start | bytes 49160 | tf_op jit(solution)/shard_map/while/body/eval_jaxpr/ppermute | solution.py:15
  133.8 6.4 %collective-permute-start.1 = (f32[64,256]{1,0:T(8,128)S(1)}, f32[64,256]{1,0:T(8,128)S(1)}, u32[]{:S(2)}, u32[]{:S(2)}) collective-permute-start(f32[64,256]{1,0:T(8,128)S(1)} %get-tuple-element.91), channel_id=1, source_target_pairs={{30,0},{0,2},{2,4},{4,6},{6,8},{8,10},{10,12},{12,14},{14,16},{16,... | collective-permute-start | bytes 196616 | tf_op jit(solution)/shard_map/while/body/eval_jaxpr/ppermute | solution.py:15
  134.3 7.7 %collective-permute-start = (f32[64,640]{1,0:T(8,128)S(1)}, f32[64,640]{1,0:T(8,128)S(1)}, u32[]{:S(2)}, u32[]{:S(2)}) collective-permute-start(f32[64,640]{1,0:T(8,128)S(1)} %get-tuple-element.89), channel_id=1, source_target_pairs={{30,0},{0,2},{2,4},{4,6},{6,8},{8,10},{10,12},{12,14},{14,16},{16,... | collective-permute-start | bytes 491528 | tf_op jit(solution)/shard_map/while/body/eval_jaxpr/ppermute | solution.py:15
  135.0 7.4 %collective-permute-start.2 = (f32[64,64]{1,0:T(8,128)S(1)}, f32[64,64]{1,0:T(8,128)S(1)}, u32[]{:S(2)}, u32[]{:S(2)}) collective-permute-start(f32[64,64]{1,0:T(8,128)S(1)} %get-tuple-element.94), channel_id=1, source_target_pairs={{30,0},{0,2},{2,4},{4,6},{6,8},{8,10},{10,12},{12,14},{14,16},{16,... | collective-permute-start | bytes 49160 | tf_op jit(solution)/shard_map/while/body/eval_jaxpr/ppermute | solution.py:15
  198.1 6.4 %collective-permute-start.1 = (f32[64,256]{1,0:T(8,128)S(1)}, f32[64,256]{1,0:T(8,128)S(1)}, u32[]{:S(2)}, u32[]{:S(2)}) collective-permute-start(f32[64,256]{1,0:T(8,128)S(1)} %get-tuple-element.91), channel_id=1, source_target_pairs={{30,0},{0,2},{2,4},{4,6},{6,8},{8,10},{10,12},{12,14},{14,16},{16,... | collective-permute-start | bytes 196616 | tf_op jit(solution)/shard_map/while/body/eval_jaxpr/ppermute | solution.py:15
  198.6 7.7 %collective-permute-start = (f32[64,640]{1,0:T(8,128)S(1)}, f32[64,640]{1,0:T(8,128)S(1)}, u32[]{:S(2)}, u32[]{:S(2)}) collective-permute-start(f32[64,640]{1,0:T(8,128)S(1)} %get-tuple-element.89), channel_id=1, source_target_pairs={{30,0},{0,2},{2,4},{4,6},{6,8},{8,10},{10,12},{12,14},{14,16},{16,... | collective-permute-start | bytes 491528 | tf_op jit(solution)/shard_map/while/body/eval_jaxpr/ppermute | solution.py:15
  199.2 7.4 %collective-permute-start.2 = (f32[64,64]{1,0:T(8,128)S(1)}, f32[64,64]{1,0:T(8,128)S(1)}, u32[]{:S(2)}, u32[]{:S(2)}) collective-permute-start(f32[64,64]{1,0:T(8,128)S(1)} %get-tuple-element.94), channel_id=1, source_target_pairs={{30,0},{0,2},{2,4},{4,6},{6,8},{8,10},{10,12},{12,14},{14,16},{16,... | collective-permute-start | bytes 49160 | tf_op jit(solution)/shard_map/while/body/eval_jaxpr/ppermute | solution.py:15
  263.3 6.4 %collective-permute-start.1 = (f32[64,256]{1,0:T(8,128)S(1)}, f32[64,256]{1,0:T(8,128)S(1)}, u32[]{:S(2)}, u32[]{:S(2)}) collective-permute-start(f32[64,256]{1,0:T(8,128)S(1)} %get-tuple-element.91), channel_id=1, source_target_pairs={{30,0},{0,2},{2,4},{4,6},{6,8},{8,10},{10,12},{12,14},{14,16},{16,... | collective-permute-start | bytes 196616 | tf_op jit(solution)/shard_map/while/body/eval_jaxpr/ppermute | solution.py:15
  263.8 7.7 %collective-permute-start = (f32[64,640]{1,0:T(8,128)S(1)}, f32[64,640]{1,0:T(8,128)S(1)}, u32[]{:S(2)}, u32[]{:S(2)}) collective-permute-start(f32[64,640]{1,0:T(8,128)S(1)} %get-tuple-element.89), channel_id=1, source_target_pairs={{30,0},{0,2},{2,4},{4,6},{6,8},{8,10},{10,12},{12,14},{14,16},{16,... | collective-permute-start | bytes 491528 | tf_op jit(solution)/shard_map/while/body/eval_jaxpr/ppermute | solution.py:15
  264.5 7.4 %collective-permute-start.2 = (f32[64,64]{1,0:T(8,128)S(1)}, f32[64,64]{1,0:T(8,128)S(1)}, u32[]{:S(2)}, u32[]{:S(2)}) collective-permute-start(f32[64,64]{1,0:T(8,128)S(1)} %get-tuple-element.94), channel_id=1, source_target_pairs={{30,0},{0,2},{2,4},{4,6},{6,8},{8,10},{10,12},{12,14},{14,16},{16,... | collective-permute-start | bytes 49160 | tf_op jit(solution)/shard_map/while/body/eval_jaxpr/ppermute | solution.py:15
  327.6 6.4 %collective-permute-start.1 = (f32[64,256]{1,0:T(8,128)S(1)}, f32[64,256]{1,0:T(8,128)S(1)}, u32[]{:S(2)}, u32[]{:S(2)}) collective-permute-start(f32[64,256]{1,0:T(8,128)S(1)} %get-tuple-element.91), channel_id=1, source_target_pairs={{30,0},{0,2},{2,4},{4,6},{6,8},{8,10},{10,12},{12,14},{14,16},{16,... | collective-permute-start | bytes 196616 | tf_op jit(solution)/shard_map/while/body/eval_jaxpr/ppermute | solution.py:15
  328.1 7.7 %collective-permute-start = (f32[64,640]{1,0:T(8,128)S(1)}, f32[64,640]{1,0:T(8,128)S(1)}, u32[]{:S(2)}, u32[]{:S(2)}) collective-permute-start(f32[64,640]{1,0:T(8,128)S(1)} %get-tuple-element.89), channel_id=1, source_target_pairs={{30,0},{0,2},{2,4},{4,6},{6,8},{8,10},{10,12},{12,14},{14,16},{16,... | collective-permute-start | bytes 491528 | tf_op jit(solution)/shard_map/while/body/eval_jaxpr/ppermute | solution.py:15
  328.8 7.4 %collective-permute-start.2 = (f32[64,64]{1,0:T(8,128)S(1)}, f32[64,64]{1,0:T(8,128)S(1)}, u32[]{:S(2)}, u32[]{:S(2)}) collective-permute-start(f32[64,64]{1,0:T(8,128)S(1)} %get-tuple-element.94), channel_id=1, source_target_pairs={{30,0},{0,2},{2,4},{4,6},{6,8},{8,10},{10,12},{12,14},{14,16},{16,... | collective-permute-start | bytes 49160 | tf_op jit(solution)/shard_map/while/body/eval_jaxpr/ppermute | solution.py:15
  392.8 6.4 %collective-permute-start.1 = (f32[64,256]{1,0:T(8,128)S(1)}, f32[64,256]{1,0:T(8,128)S(1)}, u32[]{:S(2)}, u32[]{:S(2)}) collective-permute-start(f32[64,256]{1,0:T(8,128)S(1)} %get-tuple-element.91), channel_id=1, source_target_pairs={{30,0},{0,2},{2,4},{4,6},{6,8},{8,10},{10,12},{12,14},{14,16},{16,... | collective-permute-start | bytes 196616 | tf_op jit(solution)/shard_map/while/body/eval_jaxpr/ppermute | solution.py:15
  393.4 7.7 %collective-permute-start = (f32[64,640]{1,0:T(8,128)S(1)}, f32[64,640]{1,0:T(8,128)S(1)}, u32[]{:S(2)}, u32[]{:S(2)}) collective-permute-start(f32[64,640]{1,0:T(8,128)S(1)} %get-tuple-element.89), channel_id=1, source_target_pairs={{30,0},{0,2},{2,4},{4,6},{6,8},{8,10},{10,12},{12,14},{14,16},{16,... | collective-permute-start | bytes 491528 | tf_op jit(solution)/shard_map/while/body/eval_jaxpr/ppermute | solution.py:15
  394.0 7.4 %collective-permute-start.2 = (f32[64,64]{1,0:T(8,128)S(1)}, f32[64,64]{1,0:T(8,128)S(1)}, u32[]{:S(2)}, u32[]{:S(2)}) collective-permute-start(f32[64,64]{1,0:T(8,128)S(1)} %get-tuple-element.94), channel_id=1, source_target_pairs={{30,0},{0,2},{2,4},{4,6},{6,8},{8,10},{10,12},{12,14},{14,16},{16,... | collective-permute-start | bytes 49160 | tf_op jit(solution)/shard_map/while/body/eval_jaxpr/ppermute | solution.py:15
  401.4 0.7 copy-start
  401.4 0.8 copy-start.1
where the time goes:
time: 403 us; the launch traced here: 402 us
  other arithmetic  275 us (68%)
  blocking collectives  57.1 us (14%)
  waiting for transfers between devices  42.6 us (11%)
  matrix products  17.9 us (4%)
  local copies, waits for them, and re-layouts  4.83 us (1%)
    another operation x36, other arithmetic, orth_factor(): jnp.linalg.cholesky(jnp.dot(square.T, square, precision=HIGHEST_PREC))  149 us
    another operation x24, other arithmetic, orth_factor(): jax.scipy.linalg.solve_triangular(lower_factor, square.T, lower=True)  126 us
    psum x6, blocking collectives, advance_cross(): lax.psum(gram_of(column_pair[:block_width], column_pair[block_width:]), '...  46.7 us
    ppermute x18, waiting for transfers between devices, shifted(): return lax.ppermute(block, axis, route)  42.6 us
    psum x1, blocking collectives, body(): lax.psum((gram_of(columns[:block_width], columns[:block_width]), gram_of(...  10.4 us
  transfers between devices with their start and end apart: 18, of which 18 were waited for; matrix products, arithmetic and copies ran while one was open for 2% of the time, Pallas kernels for 0%

commit v1 on v0

v1 whole, which is shorter than its diff:
```python
import functools

import jax
import jax.numpy as jnp
from jax import lax
from jax.experimental import pallas as pl
from jax.experimental.pallas import tpu as pltpu
from jax.sharding import PartitionSpec as P

STEPS = 6
SUB = 8
LANES = 128

HIGHEST_PREC = lax.Precision.HIGHEST


def shifted(block, axis, distance):
    size = lax.axis_size(axis)
    return lax.ppermute(block, axis, [((i - distance) % size, i) for i in range(size)])


def row_of(tile, k):
    return jnp.broadcast_to(tile[k:k + 1, :], tile.shape)


def column_of(tile, lane):
    return jnp.broadcast_to(tile[:, lane:lane + 1], tile.shape)


def tree_sum(terms):
    while len(terms) > 1:
        paired = [a + b for a, b in zip(terms[::2], terms[1::2])]
        if len(terms) % 2:
            paired.append(terms[-1])
        terms = paired
    return terms[0]


def eliminate(square, extras):
    count = len(square)
    sublane = lax.broadcasted_iota(jnp.int32, square[0].shape, 0)
    states = [list(square)] + [list(e) for e in extras]
    results = [[] for _ in states]
    for j in range(count):
        base = SUB * j
        tiles = [state[j] for state in states]
        columns = [column_of(tiles[0], base + m) for m in range(SUB)]
        scales, pivots_rows, coefficients = [], [], {}
        scale_column = None
        for k in range(SUB):
            scale = lax.rsqrt(row_of(columns[k], k))
            scales.append(scale)
            rows = [row_of(tile, k) * scale for tile in tiles]
            pivots_rows.append(rows)
            scale_column = scale if k == 0 else jnp.where(sublane == k, scale, scale_column)
            if k + 1 < SUB:
                multiplier = jnp.where(sublane > k, columns[k] * scale, 0.0)
                for m in range(k + 1, SUB):
                    coefficients[k, m] = row_of(multiplier, m)
                    columns[m] = columns[m] - multiplier * coefficients[k, m]
                tiles = [tile - multiplier * row for tile, row in zip(tiles, rows)]
        for result, tile in zip(results, tiles):
            result.append(tile * scale_column)
        for i in range(j + 1, count):
            multipliers = []
            for m in range(SUB):
                entry = column_of(states[0][i], base + m)
                for k in range(m):
                    entry = entry - multipliers[k] * coefficients[k, m]
                multipliers.append(entry * scales[m])
            for s, state in enumerate(states):
                state[i] = state[i] - tree_sum([multipliers[k] * pivots_rows[k][s] for k in range(SUB)])
    return results


def tiles_of(matrix):
    return [matrix[SUB * i:SUB * (i + 1)] for i in range(matrix.shape[0] // SUB)]


def rotation_transposed(gram):
    squared = jnp.dot(gram, gram, precision=HIGHEST_PREC)
    upper = jnp.concatenate(eliminate(tiles_of(squared), [])[0], 0)
    inner = lax.dot_general(upper, upper, (((1,), (1,)), ((), ())), precision=HIGHEST_PREC)
    return jnp.concatenate(eliminate(tiles_of(inner), [tiles_of(upper)])[1], 0)


def step_kernel(stay, moving, factor_stay, factor_moving, new_stay, new_moving, new_factor_stay, new_factor_moving):
    width = stay.shape[0]
    pair = jnp.concatenate([stay[...], moving[...]], 0)
    gram = lax.dot_general(pair, pair, (((1,), (1,)), ((), ())), precision=HIGHEST_PREC)
    turn = rotation_transposed(gram)
    rotated = jnp.dot(turn, pair, precision=HIGHEST_PREC)
    new_stay[...] = rotated[:width]
    new_moving[...] = rotated[width:]
    factor = jnp.concatenate([factor_stay[...], factor_moving[...]], 0)
    rotated_factor = jnp.dot(turn, factor, precision=HIGHEST_PREC)
    new_factor_stay[...] = rotated_factor[:width]
    new_factor_moving[...] = rotated_factor[width:]


def step(*arrays):
    return pl.pallas_call(
        step_kernel,
        out_shape=tuple(jax.ShapeDtypeStruct(a.shape, a.dtype) for a in arrays),
        name="pair_step",
    )(*arrays)


def body(columns, right_factor):
    width = columns.shape[0] // 2
    own = columns.shape[1]
    everywhere = jnp.concatenate(
        [columns] + [shifted(columns, "rows", d) for d in range(1, lax.axis_size("rows"))], 1
    )

    def advance(step_index, state):
        new = step(*state)
        return (new[0], shifted(new[1], "blk", 1), new[2], shifted(new[3], "blk", 1))

    state = (everywhere[:width], everywhere[width:], right_factor[:width], right_factor[width:])
    state = lax.fori_loop(0, STEPS, advance, state)
    return (
        jnp.concatenate([state[0][:, :own], state[1][:, :own]], 0),
        jnp.concatenate([state[2], state[3]], 0),
    )


def solution(mesh):
    return jax.shard_map(
        body,
        mesh=mesh,
        in_specs=(P("blk", "rows"), P("blk", "rows")),
        out_specs=(P("blk", "rows"), P("blk", "rows")),
        check_vma=False,
    )
```

time: 403 us -> 156 us (0.39)
  other arithmetic: 275 us -> 1.41 us
  Pallas kernels: 0 us -> 73.9 us
  blocking collectives: 57.1 us -> 0 us
  waiting for transfers between devices: 42.6 us -> 65.6 us
  matrix products: 17.9 us -> 0 us
  local copies, waits for them, and re-layouts: 4.83 us -> 9.3 us
    another operation x60 -> x0, other arithmetic: 274 us -> none  [the longest x36 149 us: orth_factor(): jnp.linalg.cholesky(jnp.dot(square.T, square, precision=HIGHEST_PREC))]
    pallas_call x0 -> x6, Pallas kernels: none -> 73.9 us  [step(): pl.pallas_call(step_kernel, out_shape=tuple((jax.ShapeDtypeStruct(a.shape...]
    psum x7 -> x0, blocking collectives: 57.1 us -> none  [the longest x6 46.7 us: advance_cross(): lax.psum(gram_of(column_pair[:block_width], column_pair[block_width:]), '...]
    ppermute x18 -> x13, waiting for transfers between devices: 42.6 us -> 65.6 us  [shifted(): lax.ppermute(block, axis, [((i - distance) % size, i) for i in range(size)])]
    dot_general x50 -> x0, matrix products: 14.5 us -> none  [the longest x18 5.25 us: rotate(): lax.dot_general(rotation_matrix, blocks, (((0,), (0,)), ((), ())), precis...]
    while x0 -> x12, local copies, waits for them, and re-layouts: none -> 8.13 us
  transfers between devices with their start and end apart: 18 -> 13, of which waited for: 18 -> 7; matrix products, arithmetic and copies ran while one was open for 2% -> 1% of each run, Pallas kernels for 0% -> 0%
where the time goes in v1:
time: 156 us
  Pallas kernels  73.9 us (47%)
  waiting for transfers between devices  65.6 us (42%)
  local copies, waits for them, and re-layouts  9.3 us (6%)
  starting transfers between devices  4.94 us (3%)
    pallas_call x6, Pallas kernels, step(): pl.pallas_call(step_kernel, out_shape=tuple((jax.ShapeDtypeStruct(a.shape...  73.9 us
    ppermute x13, waiting for transfers between devices, shifted(): lax.ppermute(block, axis, [((i - distance) % size, i) for i in range(size)])  65.6 us
    while x12, local copies, waits for them, and re-layouts  8.13 us
    ppermute x13, starting transfers between devices, shifted(): lax.ppermute(block, axis, [((i - distance) % size, i) for i in range(size)])  4.94 us
  transfers between devices with their start and end apart: 13, of which 7 were waited for; matrix products, arithmetic and copies ran while one was open for 1% of the time, Pallas kernels for 0%

profile of v1, /device:TPU:0, one launch (start us, length us, event | category | flops | bytes accessed | tf_op | source)
XLA Modules:
  0.0 155.9 jit_solution(14431770901001235781)
XLA Ops:
  0.6 3.0 %collective-permute-start.2 = (f32[128,640]{1,0:T(8,128)}, f32[128,640]{1,0:T(8,128)S(1)}, u32[]{:S(2)}, u32[]{:S(2)}) collective-permute-start(f32[128,640]{1,0:T(8,128)} %param.4), channel_id=1, source_target_pairs={{1,0},{0,1},{3,2},{2,3},{5,4},{4,5},{7,6},{6,7},{9,8},{8,9},{11,10... | collective-permute-start | bytes 983048 | tf_op jit(solution)/shard_map/ppermute | solution.py:19
  3.7 1.1 constant_dynamic-update-slice_fusion.1
  4.8 6.8 %collective-permute-done.2 = f32[128,640]{1,0:T(8,128)S(1)} collective-permute-done((f32[128,640]{1,0:T(8,128)}, f32[128,640]{1,0:T(8,128)S(1)}, u32[]{:S(2)}, u32[]{:S(2)}) %collective-permute-start.2) | collective-permute-done | bytes 327712 | tf_op jit(solution)/shard_map/ppermute | solution.py:19
  11.7 142.8 %while.16 = (s32[]{:T(128)}, f32[64,1280]{1,0:T(8,128)S(1)}, f32[64,1280]{1,0:T(8,128)S(1)}, f32[64,256]{1,0:T(8,128)S(1)}, f32[64,256]{1,0:T(8,128)S(1)}, /*index=5*/s32[]{:T(128)}) while((s32[]{:T(128)}, f32[64,1280]{1,0:T(8,128)S(1)}, f32[64,1280]{1,0:T(8,128)S(1)}, f32[64,256]{1,0:T(8,128)S(1)}, f32[64,256]{1,0:T(8,128)S(1)}, ...), condition=%wide.region_1.0_spmd, body=%wide.region_0.0_spmd.sunk | while | flops 2 | bytes 2359445 | solution.py:121
  11.7 0.7 copy.24.stay
  13.0 12.3 %pair_step.1 = (f32[64,1280]{1,0:T(8,128)S(1)}, f32[64,1280]{1,0:T(8,128)}, f32[64,256]{1,0:T(8,128)S(1)}, f32[64,256]{1,0:T(8,128)}) custom-call(f32[64,1280]{1,0:T(8,128)} %copy.24.stay, f32[64,1280]{1,0:T(8,128)S(1)} %get-tuple-element.101.moving, f32[64,256]{1,0:T(8,128)} %copy.25.factor_stay, f32[64,256]{1,0:T(8,128)S(1)} %get-tuple-element.103.factor_moving), custom_call_target="tpu_custom_call" | custom-call | tf_op jit(solution)/shard_map/while/body/eval_jaxpr/pair_step/pallas_call | solution.py:102
  25.4 1.9 %collective-permute-start.1 = (f32[64,256]{1,0:T(8,128)}, f32[64,256]{1,0:T(8,128)S(1)}, u32[]{:S(2)}, u32[]{:S(2)}) collective-permute-start(f32[64,256]{1,0:T(8,128)} %get-tuple-element.92), channel_id=1, source_target_pairs={{30,0},{0,2},{2,4},{4,6},{6,8},{8,10},{10,12},{12,14},{14,16},{16,... | collective-permute-start | bytes 196616 | tf_op jit(solution)/shard_map/while/body/eval_jaxpr/ppermute | solution.py:19
  27.2 8.2 %collective-permute-done.1 = f32[64,256]{1,0:T(8,128)S(1)} collective-permute-done((f32[64,256]{1,0:T(8,128)}, f32[64,256]{1,0:T(8,128)S(1)}, u32[]{:S(2)}, u32[]{:S(2)}) %collective-permute-start.1) | collective-permute-done | bytes 65568 | tf_op jit(solution)/shard_map/while/body/eval_jaxpr/ppermute | solution.py:19
  35.5 0.7 copy.24.stay
  36.8 12.3 %pair_step.1 = (f32[64,1280]{1,0:T(8,128)S(1)}, f32[64,1280]{1,0:T(8,128)}, f32[64,256]{1,0:T(8,128)S(1)}, f32[64,256]{1,0:T(8,128)}) custom-call(f32[64,1280]{1,0:T(8,128)} %copy.24.stay, f32[64,1280]{1,0:T(8,128)S(1)} %get-tuple-element.101.moving, f32[64,256]{1,0:T(8,128)} %copy.25.factor_stay, f32[64,256]{1,0:T(8,128)S(1)} %get-tuple-element.103.factor_moving), custom_call_target="tpu_custom_call" | custom-call | tf_op jit(solution)/shard_map/while/body/eval_jaxpr/pair_step/pallas_call | solution.py:102
  49.2 10.1 %collective-permute-done.1 = f32[64,256]{1,0:T(8,128)S(1)} collective-permute-done((f32[64,256]{1,0:T(8,128)}, f32[64,256]{1,0:T(8,128)S(1)}, u32[]{:S(2)}, u32[]{:S(2)}) %collective-permute-start.1) | collective-permute-done | bytes 65568 | tf_op jit(solution)/shard_map/while/body/eval_jaxpr/ppermute | solution.py:19
  59.3 0.7 copy.24.stay
  60.6 12.3 %pair_step.1 = (f32[64,1280]{1,0:T(8,128)S(1)}, f32[64,1280]{1,0:T(8,128)}, f32[64,256]{1,0:T(8,128)S(1)}, f32[64,256]{1,0:T(8,128)}) custom-call(f32[64,1280]{1,0:T(8,128)} %copy.24.stay, f32[64,1280]{1,0:T(8,128)S(1)} %get-tuple-element.101.moving, f32[64,256]{1,0:T(8,128)} %copy.25.factor_stay, f32[64,256]{1,0:T(8,128)S(1)} %get-tuple-element.103.factor_moving), custom_call_target="tpu_custom_call" | custom-call | tf_op jit(solution)/shard_map/while/body/eval_jaxpr/pair_step/pallas_call | solution.py:102
  72.9 10.1 %collective-permute-done.1 = f32[64,256]{1,0:T(8,128)S(1)} collective-permute-done((f32[64,256]{1,0:T(8,128)}, f32[64,256]{1,0:T(8,128)S(1)}, u32[]{:S(2)}, u32[]{:S(2)}) %collective-permute-start.1) | collective-permute-done | bytes 65568 | tf_op jit(solution)/shard_map/while/body/eval_jaxpr/ppermute | solution.py:19
  83.0 0.7 copy.24.stay
  84.4 12.3 %pair_step.1 = (f32[64,1280]{1,0:T(8,128)S(1)}, f32[64,1280]{1,0:T(8,128)}, f32[64,256]{1,0:T(8,128)S(1)}, f32[64,256]{1,0:T(8,128)}) custom-call(f32[64,1280]{1,0:T(8,128)} %copy.24.stay, f32[64,1280]{1,0:T(8,128)S(1)} %get-tuple-element.101.moving, f32[64,256]{1,0:T(8,128)} %copy.25.factor_stay, f32[64,256]{1,0:T(8,128)S(1)} %get-tuple-element.103.factor_moving), custom_call_target="tpu_custom_call" | custom-call | tf_op jit(solution)/shard_map/while/body/eval_jaxpr/pair_step/pallas_call | solution.py:102
  96.7 10.1 %collective-permute-done.1 = f32[64,256]{1,0:T(8,128)S(1)} collective-permute-done((f32[64,256]{1,0:T(8,128)}, f32[64,256]{1,0:T(8,128)S(1)}, u32[]{:S(2)}, u32[]{:S(2)}) %collective-permute-start.1) | collective-permute-done | bytes 65568 | tf_op jit(solution)/shard_map/while/body/eval_jaxpr/ppermute | solution.py:19
  106.8 0.7 copy.24.stay
  108.2 12.3 %pair_step.1 = (f32[64,1280]{1,0:T(8,128)S(1)}, f32[64,1280]{1,0:T(8,128)}, f32[64,256]{1,0:T(8,128)S(1)}, f32[64,256]{1,0:T(8,128)}) custom-call(f32[64,1280]{1,0:T(8,128)} %copy.24.stay, f32[64,1280]{1,0:T(8,128)S(1)} %get-tuple-element.101.moving, f32[64,256]{1,0:T(8,128)} %copy.25.factor_stay, f32[64,256]{1,0:T(8,128)S(1)} %get-tuple-element.103.factor_moving), custom_call_target="tpu_custom_call" | custom-call | tf_op jit(solution)/shard_map/while/body/eval_jaxpr/pair_step/pallas_call | solution.py:102
  120.5 10.1 %collective-permute-done.1 = f32[64,256]{1,0:T(8,128)S(1)} collective-permute-done((f32[64,256]{1,0:T(8,128)}, f32[64,256]{1,0:T(8,128)S(1)}, u32[]{:S(2)}, u32[]{:S(2)}) %collective-permute-start.1) | collective-permute-done | bytes 65568 | tf_op jit(solution)/shard_map/while/body/eval_jaxpr/ppermute | solution.py:19
  130.6 0.7 copy.24.stay
  132.0 12.3 %pair_step.1 = (f32[64,1280]{1,0:T(8,128)S(1)}, f32[64,1280]{1,0:T(8,128)}, f32[64,256]{1,0:T(8,128)S(1)}, f32[64,256]{1,0:T(8,128)}) custom-call(f32[64,1280]{1,0:T(8,128)} %copy.24.stay, f32[64,1280]{1,0:T(8,128)S(1)} %get-tuple-element.101.moving, f32[64,256]{1,0:T(8,128)} %copy.25.factor_stay, f32[64,256]{1,0:T(8,128)S(1)} %get-tuple-element.103.factor_moving), custom_call_target="tpu_custom_call" | custom-call | tf_op jit(solution)/shard_map/while/body/eval_jaxpr/pair_step/pallas_call | solution.py:102
  144.3 10.1 %collective-permute-done.1 = f32[64,256]{1,0:T(8,128)S(1)} collective-permute-done((f32[64,256]{1,0:T(8,128)}, f32[64,256]{1,0:T(8,128)S(1)}, u32[]{:S(2)}, u32[]{:S(2)}) %collective-permute-start.1) | collective-permute-done | bytes 65568 | tf_op jit(solution)/shard_map/while/body/eval_jaxpr/ppermute | solution.py:19
  155.1 0.7 pad_maximum_fusion
  (31 shorter events, 4.6 us)
Async XLA Ops:
  0.6 11.0 %collective-permute-start.2 = (f32[128,640]{1,0:T(8,128)}, f32[128,640]{1,0:T(8,128)S(1)}, u32[]{:S(2)}, u32[]{:S(2)}) collective-permute-start(f32[128,640]{1,0:T(8,128)} %param.4), channel_id=1, source_target_pairs={{1,0},{0,1},{3,2},{2,3},{5,4},{4,5},{7,6},{6,7},{9,8},{8,9},{11,10... | collective-permute-start | bytes 983048 | tf_op jit(solution)/shard_map/ppermute | solution.py:19
  3.7 1.1 copy-start
  25.4 10.1 %collective-permute-start = (f32[64,1280]{1,0:T(8,128)}, f32[64,1280]{1,0:T(8,128)S(1)}, u32[]{:S(2)}, u32[]{:S(2)}) collective-permute-start(f32[64,1280]{1,0:T(8,128)} %get-tuple-element.90), channel_id=1, source_target_pairs={{30,0},{0,2},{2,4},{4,6},{6,8},{8,10},{10,12},{12,14},{14,16},{16,... | collective-permute-start | bytes 983048 | tf_op jit(solution)/shard_map/while/body/eval_jaxpr/ppermute | solution.py:19
  25.4 10.1 %collective-permute-start.1 = (f32[64,256]{1,0:T(8,128)}, f32[64,256]{1,0:T(8,128)S(1)}, u32[]{:S(2)}, u32[]{:S(2)}) collective-permute-start(f32[64,256]{1,0:T(8,128)} %get-tuple-element.92), channel_id=1, source_target_pairs={{30,0},{0,2},{2,4},{4,6},{6,8},{8,10},{10,12},{12,14},{14,16},{16,... | collective-permute-start | bytes 196616 | tf_op jit(solution)/shard_map/while/body/eval_jaxpr/ppermute | solution.py:19
  49.1 10.1 %collective-permute-start = (f32[64,1280]{1,0:T(8,128)}, f32[64,1280]{1,0:T(8,128)S(1)}, u32[]{:S(2)}, u32[]{:S(2)}) collective-permute-start(f32[64,1280]{1,0:T(8,128)} %get-tuple-element.90), channel_id=1, source_target_pairs={{30,0},{0,2},{2,4},{4,6},{6,8},{8,10},{10,12},{12,14},{14,16},{16,... | collective-permute-start | bytes 983048 | tf_op jit(solution)/shard_map/while/body/eval_jaxpr/ppermute | solution.py:19
  49.1 10.1 %collective-permute-start.1 = (f32[64,256]{1,0:T(8,128)}, f32[64,256]{1,0:T(8,128)S(1)}, u32[]{:S(2)}, u32[]{:S(2)}) collective-permute-start(f32[64,256]{1,0:T(8,128)} %get-tuple-element.92), channel_id=1, source_target_pairs={{30,0},{0,2},{2,4},{4,6},{6,8},{8,10},{10,12},{12,14},{14,16},{16,... | collective-permute-start | bytes 196616 | tf_op jit(solution)/shard_map/while/body/eval_jaxpr/ppermute | solution.py:19
  72.9 10.1 %collective-permute-start = (f32[64,1280]{1,0:T(8,128)}, f32[64,1280]{1,0:T(8,128)S(1)}, u32[]{:S(2)}, u32[]{:S(2)}) collective-permute-start(f32[64,1280]{1,0:T(8,128)} %get-tuple-element.90), channel_id=1, source_target_pairs={{30,0},{0,2},{2,4},{4,6},{6,8},{8,10},{10,12},{12,14},{14,16},{16,... | collective-permute-start | bytes 983048 | tf_op jit(solution)/shard_map/while/body/eval_jaxpr/ppermute | solution.py:19
  72.9 10.1 %collective-permute-start.1 = (f32[64,256]{1,0:T(8,128)}, f32[64,256]{1,0:T(8,128)S(1)}, u32[]{:S(2)}, u32[]{:S(2)}) collective-permute-start(f32[64,256]{1,0:T(8,128)} %get-tuple-element.92), channel_id=1, source_target_pairs={{30,0},{0,2},{2,4},{4,6},{6,8},{8,10},{10,12},{12,14},{14,16},{16,... | collective-permute-start | bytes 196616 | tf_op jit(solution)/shard_map/while/body/eval_jaxpr/ppermute | solution.py:19
  96.7 10.1 %collective-permute-start = (f32[64,1280]{1,0:T(8,128)}, f32[64,1280]{1,0:T(8,128)S(1)}, u32[]{:S(2)}, u32[]{:S(2)}) collective-permute-start(f32[64,1280]{1,0:T(8,128)} %get-tuple-element.90), channel_id=1, source_target_pairs={{30,0},{0,2},{2,4},{4,6},{6,8},{8,10},{10,12},{12,14},{14,16},{16,... | collective-permute-start | bytes 983048 | tf_op jit(solution)/shard_map/while/body/eval_jaxpr/ppermute | solution.py:19
  96.7 10.1 %collective-permute-start.1 = (f32[64,256]{1,0:T(8,128)}, f32[64,256]{1,0:T(8,128)S(1)}, u32[]{:S(2)}, u32[]{:S(2)}) collective-permute-start(f32[64,256]{1,0:T(8,128)} %get-tuple-element.92), channel_id=1, source_target_pairs={{30,0},{0,2},{2,4},{4,6},{6,8},{8,10},{10,12},{12,14},{14,16},{16,... | collective-permute-start | bytes 196616 | tf_op jit(solution)/shard_map/while/body/eval_jaxpr/ppermute | solution.py:19
  120.5 10.1 %collective-permute-start = (f32[64,1280]{1,0:T(8,128)}, f32[64,1280]{1,0:T(8,128)S(1)}, u32[]{:S(2)}, u32[]{:S(2)}) collective-permute-start(f32[64,1280]{1,0:T(8,128)} %get-tuple-element.90), channel_id=1, source_target_pairs={{30,0},{0,2},{2,4},{4,6},{6,8},{8,10},{10,12},{12,14},{14,16},{16,... | collective-permute-start | bytes 983048 | tf_op jit(solution)/shard_map/while/body/eval_jaxpr/ppermute | solution.py:19
  120.5 10.1 %collective-permute-start.1 = (f32[64,256]{1,0:T(8,128)}, f32[64,256]{1,0:T(8,128)S(1)}, u32[]{:S(2)}, u32[]{:S(2)}) collective-permute-start(f32[64,256]{1,0:T(8,128)} %get-tuple-element.92), channel_id=1, source_target_pairs={{30,0},{0,2},{2,4},{4,6},{6,8},{8,10},{10,12},{12,14},{14,16},{16,... | collective-permute-start | bytes 196616 | tf_op jit(solution)/shard_map/while/body/eval_jaxpr/ppermute | solution.py:19
  144.3 10.1 %collective-permute-start = (f32[64,1280]{1,0:T(8,128)}, f32[64,1280]{1,0:T(8,128)S(1)}, u32[]{:S(2)}, u32[]{:S(2)}) collective-permute-start(f32[64,1280]{1,0:T(8,128)} %get-tuple-element.90), channel_id=1, source_target_pairs={{30,0},{0,2},{2,4},{4,6},{6,8},{8,10},{10,12},{12,14},{14,16},{16,... | collective-permute-start | bytes 983048 | tf_op jit(solution)/shard_map/while/body/eval_jaxpr/ppermute | solution.py:19
  144.3 10.1 %collective-permute-start.1 = (f32[64,256]{1,0:T(8,128)}, f32[64,256]{1,0:T(8,128)S(1)}, u32[]{:S(2)}, u32[]{:S(2)}) collective-permute-start(f32[64,256]{1,0:T(8,128)} %get-tuple-element.92), channel_id=1, source_target_pairs={{30,0},{0,2},{2,4},{4,6},{6,8},{8,10},{10,12},{12,14},{14,16},{16,... | collective-permute-start | bytes 196616 | tf_op jit(solution)/shard_map/while/body/eval_jaxpr/ppermute | solution.py:19

commit v2 on v1

--- a/solution.py
+++ b/solution.py
@@ -9,7 +9,7 @@
 
 STEPS = 6
 SUB = 8
-LANES = 128
+KERNEL_PARAMS = pltpu.CompilerParams(vmem_limit_bytes=24 * 1024 * 1024)
 
 HIGHEST_PREC = lax.Precision.HIGHEST
 
@@ -84,26 +84,55 @@
     return jnp.concatenate(eliminate(tiles_of(inner), [tiles_of(upper)])[1], 0)
 
 
-def step_kernel(stay, moving, factor_stay, factor_moving, new_stay, new_moving, new_factor_stay, new_factor_moving):
-    width = stay.shape[0]
-    pair = jnp.concatenate([stay[...], moving[...]], 0)
-    gram = lax.dot_general(pair, pair, (((1,), (1,)), ((), ())), precision=HIGHEST_PREC)
-    turn = rotation_transposed(gram)
-    rotated = jnp.dot(turn, pair, precision=HIGHEST_PREC)
-    new_stay[...] = rotated[:width]
-    new_moving[...] = rotated[width:]
-    factor = jnp.concatenate([factor_stay[...], factor_moving[...]], 0)
-    rotated_factor = jnp.dot(turn, factor, precision=HIGHEST_PREC)
-    new_factor_stay[...] = rotated_factor[:width]
-    new_factor_moving[...] = rotated_factor[width:]
+def split(values):
+    high = values.astype(jnp.bfloat16)
+    return high, (values - high.astype(jnp.float32)).astype(jnp.bfloat16)
 
 
-def step(*arrays):
+def three_pass(left, right, dims):
+    left_high, left_low = split(left)
+    right_high, right_low = split(right)
+
+    def product(a, b):
+        return lax.dot_general(a, b, (dims, ((), ())), preferred_element_type=jnp.float32)
+
+    return product(left_high, right_high) + (product(left_high, right_low) + product(left_low, right_high))
+
+
+def turn_kernel(stay, moving, turn):
+    pair = jnp.concatenate([stay[...], moving[...]], 0)
+    turn[...] = rotation_transposed(three_pass(pair, pair, ((1,), (1,))))
+
+
+def rotate_kernel(turn, upper, lower, factor_upper, factor_lower, *outputs):
+    columns = jnp.concatenate([upper[...], lower[...]], 0)
+    factor = jnp.concatenate([factor_upper[...], factor_lower[...]], 0)
+    width = upper.shape[0]
+    for index in range(len(outputs) // 2):
+        rows = turn[width * index:width * (index + 1), :]
+        outputs[2 * index][...] = three_pass(rows, columns, ((1,), (0,)))
+        outputs[2 * index + 1][...] = three_pass(rows, factor, ((1,), (0,)))
+
+
+def find_turn(stay, moving):
+    size = 2 * stay.shape[0]
     return pl.pallas_call(
-        step_kernel,
-        out_shape=tuple(jax.ShapeDtypeStruct(a.shape, a.dtype) for a in arrays),
-        name="pair_step",
-    )(*arrays)
+        turn_kernel,
+        out_shape=jax.ShapeDtypeStruct((size, size), stay.dtype),
+        compiler_params=KERNEL_PARAMS,
+        name="find_turn",
+    )(stay, moving)
+
+
+def rotate(turn, upper, lower, factor_upper, factor_lower, halves):
+    shapes = [jax.ShapeDtypeStruct(a.shape, a.dtype) for a in (upper, factor_upper)]
+    return pl.pallas_call(
+        rotate_kernel,
+        out_shape=tuple(shapes * halves),
+        input_output_aliases={1: 0, 3: 1},
+        compiler_params=KERNEL_PARAMS,
+        name=f"rotate_{halves}",
+    )(turn, upper, lower, factor_upper, factor_lower)
 
 
 def body(columns, right_factor):
@@ -114,14 +143,25 @@
     )
 
     def advance(step_index, state):
-        new = step(*state)
-        return (new[0], shifted(new[1], "blk", 1), new[2], shifted(new[3], "blk", 1))
+        stay, moving, near_stay, factor_stay, factor_moving, near_factor_stay = state
+        near_moving = shifted(moving, "blk", 1)
+        near_factor_moving = shifted(factor_moving, "blk", 1)
+        turn = find_turn(stay, moving)
+        near_turn = shifted(turn, "blk", 1)
+        stay, factor_stay = rotate(turn, stay, moving, factor_stay, factor_moving, 1)
+        near_stay, near_factor_stay, moving, factor_moving = rotate(
+            near_turn, near_stay, near_moving, near_factor_stay, near_factor_moving, 2
+        )
+        return stay, moving, near_stay, factor_stay, factor_moving, near_factor_stay
 
-    state = (everywhere[:width], everywhere[width:], right_factor[:width], right_factor[width:])
-    state = lax.fori_loop(0, STEPS, advance, state)
+    state = (
+        everywhere[:width], everywhere[width:], shifted(everywhere[:width], "blk", 1),
+        right_factor[:width], right_factor[width:], shifted(right_factor[:width], "blk", 1),
+    )
+    stay, moving, _, factor_stay, factor_moving, _ = lax.fori_loop(0, STEPS, advance, state)
     return (
-        jnp.concatenate([state[0][:, :own], state[1][:, :own]], 0),
-        jnp.concatenate([state[2], state[3]], 0),
+        jnp.concatenate([stay[:, :own], moving[:, :own]], 0),
+        jnp.concatenate([factor_stay, factor_moving], 0),
     )
 
 

time: 156 us -> 119 us (0.76)
  Pallas kernels: 73.9 us -> 58.7 us
  waiting for transfers between devices: 65.6 us -> 51 us
  local copies, waits for them, and re-layouts: 9.3 us -> 1.91 us
    pallas_call x6 -> x18, Pallas kernels: 73.9 us -> 58.7 us  [the longest x6 53.8 us: find_turn(): pl.pallas_call(turn_kernel, out_shape=jax.ShapeDtypeStruct((size, size),...]
    ppermute x13 -> x21, waiting for transfers between devices: 65.6 us -> 51 us  [shifted(): lax.ppermute(block, axis, [((i - distance) % size, i) for i in range(size)])]
    while x12 -> x0, local copies, waits for them, and re-layouts: 8.13 us -> none
    ppermute x13 -> x21, starting transfers between devices: 4.94 us -> 5.17 us  [shifted(): lax.ppermute(block, axis, [((i - distance) % size, i) for i in range(size)])]
  transfers between devices with their start and end apart: 13 -> 21, of which waited for: 7 -> 14; matrix products, arithmetic and copies ran while one was open for 1% -> 1% of each run, Pallas kernels for 0% -> 47%
where the time goes in v2:
time: 119 us
  Pallas kernels  58.7 us (49%)
  waiting for transfers between devices  51 us (43%)
  starting transfers between devices  5.17 us (4%)
  local copies, waits for them, and re-layouts  1.91 us (2%)
  other arithmetic  1.41 us (1%)
    pallas_call x6, Pallas kernels, find_turn(): pl.pallas_call(turn_kernel, out_shape=jax.ShapeDtypeStruct((size, size),...  53.8 us
    ppermute x21, waiting for transfers between devices, shifted(): lax.ppermute(block, axis, [((i - distance) % size, i) for i in range(size)])  51 us
    ppermute x21, starting transfers between devices, shifted(): lax.ppermute(block, axis, [((i - distance) % size, i) for i in range(size)])  5.17 us
    pallas_call x12, Pallas kernels, rotate(): pl.pallas_call(rotate_kernel, out_shape=tuple(shapes * halves), input_out...  4.9 us
  transfers between devices with their start and end apart: 21, of which 14 were waited for; matrix products, arithmetic and copies ran while one was open for 1% of the time, Pallas kernels for 47%

profile of v2, /device:TPU:0, one launch (start us, length us, event | category | flops | bytes accessed | tf_op | source)
XLA Modules:
  0.0 119.3 jit_solution(9567214200242809051)
XLA Ops:
  0.6 3.0 %collective-permute-start.3 = (f32[128,640]{1,0:T(8,128)}, f32[128,640]{1,0:T(8,128)S(1)}, u32[]{:S(2)}, u32[]{:S(2)}) collective-permute-start(f32[128,640]{1,0:T(8,128)} %param.4), channel_id=1, source_target_pairs={{1,0},{0,1},{3,2},{2,3},{5,4},{4,5},{7,6},{6,7},{9,8},{8,9},{11,10... | collective-permute-start | bytes 983048 | tf_op jit(solution)/shard_map/ppermute | solution.py:19
  3.7 1.0 constant_dynamic-update-slice_fusion.1
  4.7 6.9 %collective-permute-done.3 = f32[128,640]{1,0:T(8,128)S(1)} collective-permute-done((f32[128,640]{1,0:T(8,128)}, f32[128,640]{1,0:T(8,128)S(1)}, u32[]{:S(2)}, u32[]{:S(2)}) %collective-permute-start.3) | collective-permute-done | bytes 327712 | tf_op jit(solution)/shard_map/ppermute | solution.py:19
  11.7 0.8 copy-done
  12.5 1.1 collective-permute-start.5
  13.7 7.9 %collective-permute-done.5 = f32[64,256]{1,0:T(8,128)S(1)} collective-permute-done((f32[64,256]{1,0:T(8,128)S(1)}, f32[64,256]{1,0:T(8,128)S(1)}, u32[]{:S(2)}, u32[]{:S(2)}) %collective-permute-start.5) | collective-permute-done | bytes 65568 | tf_op jit(solution)/shard_map/ppermute | solution.py:19
  21.6 96.2 %while.20 = (s32[]{:T(128)}, f32[64,1280]{1,0:T(8,128)S(1)}, f32[64,1280]{1,0:T(8,128)S(1)}, f32[64,1280]{1,0:T(8,128)S(1)}, f32[64,256]{1,0:T(8,128)S(1)}, /*in...) while((s32[]{:T(128)}, f32[64,1280]{1,0:T(8,128)S(1)}, f32[64,1280]{1,0:T(8,128)S(1)}, ...), condition=%wide.region_1.0_spmd, body=%wide.region_0.0_spmd.sunk | while | flops 2 | bytes 1835213 | solution.py:161
  21.6 9.0 %find_turn.1.turn = f32[128,128]{1,0:T(8,128)S(1)} custom-call(f32[64,1280]{1,0:T(8,128)S(1)} %get-tuple-element.134.stay.upper, f32[64,1280]{1,0:T(8,128)S(1)} %get-tuple-element.135.moving.lower), custom_call_target="tpu_custom_call" | custom-call | tf_op jit(solution)/shard_map/while/body/eval_jaxpr/find_turn/pallas_call | solution.py:119
  31.0 0.5 collective-permute-done.2.factor_lower
  31.5 5.5 %collective-permute-done.turn = f32[128,128]{1,0:T(8,128)S(1)} collective-permute-done((f32[128,128]{1,0:T(8,128)S(1)}, f32[128,128]{1,0:T(8,128)S(1)}, u32[]{:S(2)}, u32[]{:S(2)}) %collective-permute-start) | collective-permute-done | bytes 65568 | tf_op jit(solution)/shard_map/while/body/eval_jaxpr/ppermute | solution.py:19
  37.7 9.0 %find_turn.1.turn = f32[128,128]{1,0:T(8,128)S(1)} custom-call(f32[64,1280]{1,0:T(8,128)S(1)} %get-tuple-element.134.stay.upper, f32[64,1280]{1,0:T(8,128)S(1)} %get-tuple-element.135.moving.lower), custom_call_target="tpu_custom_call" | custom-call | tf_op jit(solution)/shard_map/while/body/eval_jaxpr/find_turn/pallas_call | solution.py:119
  47.5 5.6 %collective-permute-done.turn = f32[128,128]{1,0:T(8,128)S(1)} collective-permute-done((f32[128,128]{1,0:T(8,128)S(1)}, f32[128,128]{1,0:T(8,128)S(1)}, u32[]{:S(2)}, u32[]{:S(2)}) %collective-permute-start) | collective-permute-done | bytes 65568 | tf_op jit(solution)/shard_map/while/body/eval_jaxpr/ppermute | solution.py:19
  53.1 0.5 rotate_2.1
  53.8 9.0 %find_turn.1.turn = f32[128,128]{1,0:T(8,128)S(1)} custom-call(f32[64,1280]{1,0:T(8,128)S(1)} %get-tuple-element.134.stay.upper, f32[64,1280]{1,0:T(8,128)S(1)} %get-tuple-element.135.moving.lower), custom_call_target="tpu_custom_call" | custom-call | tf_op jit(solution)/shard_map/while/body/eval_jaxpr/find_turn/pallas_call | solution.py:119
  63.6 5.6 %collective-permute-done.turn = f32[128,128]{1,0:T(8,128)S(1)} collective-permute-done((f32[128,128]{1,0:T(8,128)S(1)}, f32[128,128]{1,0:T(8,128)S(1)}, u32[]{:S(2)}, u32[]{:S(2)}) %collective-permute-start) | collective-permute-done | bytes 65568 | tf_op jit(solution)/shard_map/while/body/eval_jaxpr/ppermute | solution.py:19
  69.8 9.0 %find_turn.1.turn = f32[128,128]{1,0:T(8,128)S(1)} custom-call(f32[64,1280]{1,0:T(8,128)S(1)} %get-tuple-element.134.stay.upper, f32[64,1280]{1,0:T(8,128)S(1)} %get-tuple-element.135.moving.lower), custom_call_target="tpu_custom_call" | custom-call | tf_op jit(solution)/shard_map/while/body/eval_jaxpr/find_turn/pallas_call | solution.py:119
  79.6 5.6 %collective-permute-done.turn = f32[128,128]{1,0:T(8,128)S(1)} collective-permute-done((f32[128,128]{1,0:T(8,128)S(1)}, f32[128,128]{1,0:T(8,128)S(1)}, u32[]{:S(2)}, u32[]{:S(2)}) %collective-permute-start) | collective-permute-done | bytes 65568 | tf_op jit(solution)/shard_map/while/body/eval_jaxpr/ppermute | solution.py:19
  85.9 9.0 %find_turn.1.turn = f32[128,128]{1,0:T(8,128)S(1)} custom-call(f32[64,1280]{1,0:T(8,128)S(1)} %get-tuple-element.134.stay.upper, f32[64,1280]{1,0:T(8,128)S(1)} %get-tuple-element.135.moving.lower), custom_call_target="tpu_custom_call" | custom-call | tf_op jit(solution)/shard_map/while/body/eval_jaxpr/find_turn/pallas_call | solution.py:119
  95.7 5.6 %collective-permute-done.turn = f32[128,128]{1,0:T(8,128)S(1)} collective-permute-done((f32[128,128]{1,0:T(8,128)S(1)}, f32[128,128]{1,0:T(8,128)S(1)}, u32[]{:S(2)}, u32[]{:S(2)}) %collective-permute-start) | collective-permute-done | bytes 65568 | tf_op jit(solution)/shard_map/while/body/eval_jaxpr/ppermute | solution.py:19
  101.3 0.5 rotate_2.1
  101.9 9.0 %find_turn.1.turn = f32[128,128]{1,0:T(8,128)S(1)} custom-call(f32[64,1280]{1,0:T(8,128)S(1)} %get-tuple-element.134.stay.upper, f32[64,1280]{1,0:T(8,128)S(1)} %get-tuple-element.135.moving.lower), custom_call_target="tpu_custom_call" | custom-call | tf_op jit(solution)/shard_map/while/body/eval_jaxpr/find_turn/pallas_call | solution.py:119
  111.7 5.6 %collective-permute-done.turn = f32[128,128]{1,0:T(8,128)S(1)} collective-permute-done((f32[128,128]{1,0:T(8,128)S(1)}, f32[128,128]{1,0:T(8,128)S(1)}, u32[]{:S(2)}, u32[]{:S(2)}) %collective-permute-start) | collective-permute-done | bytes 65568 | tf_op jit(solution)/shard_map/while/body/eval_jaxpr/ppermute | solution.py:19
  117.9 0.7 pad_maximum_fusion.1
  118.5 0.7 pad_maximum_fusion
  (47 shorter events, 7.2 us)
Async XLA Ops:
  0.6 11.0 %collective-permute-start.3 = (f32[128,640]{1,0:T(8,128)}, f32[128,640]{1,0:T(8,128)S(1)}, u32[]{:S(2)}, u32[]{:S(2)}) collective-permute-start(f32[128,640]{1,0:T(8,128)} %param.4), channel_id=1, source_target_pairs={{1,0},{0,1},{3,2},{2,3},{5,4},{4,5},{7,6},{6,7},{9,8},{8,9},{11,10... | collective-permute-start | bytes 983048 | tf_op jit(solution)/shard_map/ppermute | solution.py:19
  11.6 0.9 copy-start
  11.7 10.0 %collective-permute-start.4 = (f32[64,1280]{1,0:T(8,128)S(1)}, f32[64,1280]{1,0:T(8,128)S(1)}, u32[]{:S(2)}, u32[]{:S(2)}) collective-permute-start(f32[64,1280]{1,0:T(8,128)S(1)} %get-tuple-element.126), channel_id=1, source_target_pairs={{30,0},{0,2},{2,4},{4,6},{6,8},{8,10},{10,12},{12,14},{14,16},{16,... | collective-permute-start | bytes 983048 | tf_op jit(solution)/shard_map/ppermute | solution.py:19
  12.5 9.1 %collective-permute-start.5 = (f32[64,256]{1,0:T(8,128)S(1)}, f32[64,256]{1,0:T(8,128)S(1)}, u32[]{:S(2)}, u32[]{:S(2)}) collective-permute-start(f32[64,256]{1,0:T(8,128)S(1)} %get-tuple-element.129), channel_id=1, source_target_pairs={{30,0},{0,2},{2,4},{4,6},{6,8},{8,10},{10,12},{12,14},{14,16},{16,... | collective-permute-start | bytes 196616 | tf_op jit(solution)/shard_map/ppermute | solution.py:19
  21.6 15.4 %collective-permute-start.1 = (f32[64,1280]{1,0:T(8,128)S(1)}, f32[64,1280]{1,0:T(8,128)S(1)}, u32[]{:S(2)}, u32[]{:S(2)}) collective-permute-start(f32[64,1280]{1,0:T(8,128)S(1)} %get-tuple-element.135.moving.lower), channel_id=1, source_target_pairs={{30,0},{0,2},{2,4},{4,6},{6,8},{8,10},{10,12},{12,14},{14,16},{16,... | collective-permute-start | bytes 983048 | tf_op jit(solution)/shard_map/while/body/eval_jaxpr/ppermute | solution.py:19
  21.6 9.9 %collective-permute-start.2 = (f32[64,256]{1,0:T(8,128)S(1)}, f32[64,256]{1,0:T(8,128)S(1)}, u32[]{:S(2)}, u32[]{:S(2)}) collective-permute-start(f32[64,256]{1,0:T(8,128)S(1)} %get-tuple-element.138.factor_lower), channel_id=1, source_target_pairs={{30,0},{0,2},{2,4},{4,6},{6,8},{8,10},{10,12},{12,14},{14,16},{16,... | collective-permute-start | bytes 196616 | tf_op jit(solution)/shard_map/while/body/eval_jaxpr/ppermute | solution.py:19
  30.6 6.5 %collective-permute-start = (f32[128,128]{1,0:T(8,128)S(1)}, f32[128,128]{1,0:T(8,128)S(1)}, u32[]{:S(2)}, u32[]{:S(2)}) collective-permute-start(f32[128,128]{1,0:T(8,128)S(1)} %find_turn.1.turn), channel_id=1, source_target_pairs={{30,0},{0,2},{2,4},{4,6},{6,8},{8,10},{10,12},{12,14},{14,16},{16,... | collective-permute-start | bytes 196616 | tf_op jit(solution)/shard_map/while/body/eval_jaxpr/ppermute | solution.py:19
  37.6 15.5 %collective-permute-start.1 = (f32[64,1280]{1,0:T(8,128)S(1)}, f32[64,1280]{1,0:T(8,128)S(1)}, u32[]{:S(2)}, u32[]{:S(2)}) collective-permute-start(f32[64,1280]{1,0:T(8,128)S(1)} %get-tuple-element.135.moving.lower), channel_id=1, source_target_pairs={{30,0},{0,2},{2,4},{4,6},{6,8},{8,10},{10,12},{12,14},{14,16},{16,... | collective-permute-start | bytes 983048 | tf_op jit(solution)/shard_map/while/body/eval_jaxpr/ppermute | solution.py:19
  37.6 9.9 %collective-permute-start.2 = (f32[64,256]{1,0:T(8,128)S(1)}, f32[64,256]{1,0:T(8,128)S(1)}, u32[]{:S(2)}, u32[]{:S(2)}) collective-permute-start(f32[64,256]{1,0:T(8,128)S(1)} %get-tuple-element.138.factor_lower), channel_id=1, source_target_pairs={{30,0},{0,2},{2,4},{4,6},{6,8},{8,10},{10,12},{12,14},{14,16},{16,... | collective-permute-start | bytes 196616 | tf_op jit(solution)/shard_map/while/body/eval_jaxpr/ppermute | solution.py:19
  46.7 6.4 %collective-permute-start = (f32[128,128]{1,0:T(8,128)S(1)}, f32[128,128]{1,0:T(8,128)S(1)}, u32[]{:S(2)}, u32[]{:S(2)}) collective-permute-start(f32[128,128]{1,0:T(8,128)S(1)} %find_turn.1.turn), channel_id=1, source_target_pairs={{30,0},{0,2},{2,4},{4,6},{6,8},{8,10},{10,12},{12,14},{14,16},{16,... | collective-permute-start | bytes 196616 | tf_op jit(solution)/shard_map/while/body/eval_jaxpr/ppermute | solution.py:19
  53.6 15.6 %collective-permute-start.1 = (f32[64,1280]{1,0:T(8,128)S(1)}, f32[64,1280]{1,0:T(8,128)S(1)}, u32[]{:S(2)}, u32[]{:S(2)}) collective-permute-start(f32[64,1280]{1,0:T(8,128)S(1)} %get-tuple-element.135.moving.lower), channel_id=1, source_target_pairs={{30,0},{0,2},{2,4},{4,6},{6,8},{8,10},{10,12},{12,14},{14,16},{16,... | collective-permute-start | bytes 983048 | tf_op jit(solution)/shard_map/while/body/eval_jaxpr/ppermute | solution.py:19
  53.7 9.9 %collective-permute-start.2 = (f32[64,256]{1,0:T(8,128)S(1)}, f32[64,256]{1,0:T(8,128)S(1)}, u32[]{:S(2)}, u32[]{:S(2)}) collective-permute-start(f32[64,256]{1,0:T(8,128)S(1)} %get-tuple-element.138.factor_lower), channel_id=1, source_target_pairs={{30,0},{0,2},{2,4},{4,6},{6,8},{8,10},{10,12},{12,14},{14,16},{16,... | collective-permute-start | bytes 196616 | tf_op jit(solution)/shard_map/while/body/eval_jaxpr/ppermute | solution.py:19
  62.7 6.4 %collective-permute-start = (f32[128,128]{1,0:T(8,128)S(1)}, f32[128,128]{1,0:T(8,128)S(1)}, u32[]{:S(2)}, u32[]{:S(2)}) collective-permute-start(f32[128,128]{1,0:T(8,128)S(1)} %find_turn.1.turn), channel_id=1, source_target_pairs={{30,0},{0,2},{2,4},{4,6},{6,8},{8,10},{10,12},{12,14},{14,16},{16,... | collective-permute-start | bytes 196616 | tf_op jit(solution)/shard_map/while/body/eval_jaxpr/ppermute | solution.py:19
  69.7 15.6 %collective-permute-start.1 = (f32[64,1280]{1,0:T(8,128)S(1)}, f32[64,1280]{1,0:T(8,128)S(1)}, u32[]{:S(2)}, u32[]{:S(2)}) collective-permute-start(f32[64,1280]{1,0:T(8,128)S(1)} %get-tuple-element.135.moving.lower), channel_id=1, source_target_pairs={{30,0},{0,2},{2,4},{4,6},{6,8},{8,10},{10,12},{12,14},{14,16},{16,... | collective-permute-start | bytes 983048 | tf_op jit(solution)/shard_map/while/body/eval_jaxpr/ppermute | solution.py:19
  69.7 9.9 %collective-permute-start.2 = (f32[64,256]{1,0:T(8,128)S(1)}, f32[64,256]{1,0:T(8,128)S(1)}, u32[]{:S(2)}, u32[]{:S(2)}) collective-permute-start(f32[64,256]{1,0:T(8,128)S(1)} %get-tuple-element.138.factor_lower), channel_id=1, source_target_pairs={{30,0},{0,2},{2,4},{4,6},{6,8},{8,10},{10,12},{12,14},{14,16},{16,... | collective-permute-start | bytes 196616 | tf_op jit(solution)/shard_map/while/body/eval_jaxpr/ppermute | solution.py:19
  78.8 6.4 %collective-permute-start = (f32[128,128]{1,0:T(8,128)S(1)}, f32[128,128]{1,0:T(8,128)S(1)}, u32[]{:S(2)}, u32[]{:S(2)}) collective-permute-start(f32[128,128]{1,0:T(8,128)S(1)} %find_turn.1.turn), channel_id=1, source_target_pairs={{30,0},{0,2},{2,4},{4,6},{6,8},{8,10},{10,12},{12,14},{14,16},{16,... | collective-permute-start | bytes 196616 | tf_op jit(solution)/shard_map/while/body/eval_jaxpr/ppermute | solution.py:19
  85.7 15.6 %collective-permute-start.1 = (f32[64,1280]{1,0:T(8,128)S(1)}, f32[64,1280]{1,0:T(8,128)S(1)}, u32[]{:S(2)}, u32[]{:S(2)}) collective-permute-start(f32[64,1280]{1,0:T(8,128)S(1)} %get-tuple-element.135.moving.lower), channel_id=1, source_target_pairs={{30,0},{0,2},{2,4},{4,6},{6,8},{8,10},{10,12},{12,14},{14,16},{16,... | collective-permute-start | bytes 983048 | tf_op jit(solution)/shard_map/while/body/eval_jaxpr/ppermute | solution.py:19
  85.8 9.9 %collective-permute-start.2 = (f32[64,256]{1,0:T(8,128)S(1)}, f32[64,256]{1,0:T(8,128)S(1)}, u32[]{:S(2)}, u32[]{:S(2)}) collective-permute-start(f32[64,256]{1,0:T(8,128)S(1)} %get-tuple-element.138.factor_lower), channel_id=1, source_target_pairs={{30,0},{0,2},{2,4},{4,6},{6,8},{8,10},{10,12},{12,14},{14,16},{16,... | collective-permute-start | bytes 196616 | tf_op jit(solution)/shard_map/while/body/eval_jaxpr/ppermute | solution.py:19
  94.8 6.4 %collective-permute-start = (f32[128,128]{1,0:T(8,128)S(1)}, f32[128,128]{1,0:T(8,128)S(1)}, u32[]{:S(2)}, u32[]{:S(2)}) collective-permute-start(f32[128,128]{1,0:T(8,128)S(1)} %find_turn.1.turn), channel_id=1, source_target_pairs={{30,0},{0,2},{2,4},{4,6},{6,8},{8,10},{10,12},{12,14},{14,16},{16,... | collective-permute-start | bytes 196616 | tf_op jit(solution)/shard_map/while/body/eval_jaxpr/ppermute | solution.py:19
  101.8 15.6 %collective-permute-start.1 = (f32[64,1280]{1,0:T(8,128)S(1)}, f32[64,1280]{1,0:T(8,128)S(1)}, u32[]{:S(2)}, u32[]{:S(2)}) collective-permute-start(f32[64,1280]{1,0:T(8,128)S(1)} %get-tuple-element.135.moving.lower), channel_id=1, source_target_pairs={{30,0},{0,2},{2,4},{4,6},{6,8},{8,10},{10,12},{12,14},{14,16},{16,... | collective-permute-start | bytes 983048 | tf_op jit(solution)/shard_map/while/body/eval_jaxpr/ppermute | solution.py:19
  101.8 9.9 %collective-permute-start.2 = (f32[64,256]{1,0:T(8,128)S(1)}, f32[64,256]{1,0:T(8,128)S(1)}, u32[]{:S(2)}, u32[]{:S(2)}) collective-permute-start(f32[64,256]{1,0:T(8,128)S(1)} %get-tuple-element.138.factor_lower), channel_id=1, source_target_pairs={{30,0},{0,2},{2,4},{4,6},{6,8},{8,10},{10,12},{12,14},{14,16},{16,... | collective-permute-start | bytes 196616 | tf_op jit(solution)/shard_map/while/body/eval_jaxpr/ppermute | solution.py:19
  110.9 6.4 %collective-permute-start = (f32[128,128]{1,0:T(8,128)S(1)}, f32[128,128]{1,0:T(8,128)S(1)}, u32[]{:S(2)}, u32[]{:S(2)}) collective-permute-start(f32[128,128]{1,0:T(8,128)S(1)} %find_turn.1.turn), channel_id=1, source_target_pairs={{30,0},{0,2},{2,4},{4,6},{6,8},{8,10},{10,12},{12,14},{14,16},{16,... | collective-permute-start | bytes 196616 | tf_op jit(solution)/shard_map/while/body/eval_jaxpr/ppermute | solution.py:19

commit v3 on v2

v3 whole, which is shorter than its diff:
```python
import functools

import jax
import jax.numpy as jnp
from jax import lax
from jax.experimental import pallas as pl
from jax.experimental.pallas import tpu as pltpu
from jax.sharding import PartitionSpec as P


STEPS = 6
SUB = 8
KERNEL_PARAMS = pltpu.CompilerParams(vmem_limit_bytes=24 * 1024 * 1024)

HIGHEST_PREC = lax.Precision.HIGHEST


def shifted(block, axis, distance):
    size = lax.axis_size(axis)
    return lax.ppermute(block, axis, [((i - distance) % size, i) for i in range(size)])


def row_of(tile, k):
    return jnp.broadcast_to(tile[k:k + 1, :], tile.shape)


def column_of(tile, lane):
    return jnp.broadcast_to(tile[:, lane:lane + 1], tile.shape)


def tree_sum(terms):
    while len(terms) > 1:
        paired = [a + b for a, b in zip(terms[::2], terms[1::2])]
        if len(terms) % 2:
            paired.append(terms[-1])
        terms = paired
    return terms[0]


def sweep(square, extras):
    count = len(square)
    sublane = lax.broadcasted_iota(jnp.int32, square[0].shape, 0)
    below = [sublane > k for k in range(SUB)]
    states = [list(square)] + [list(e) for e in extras]
    results = [[] for _ in states]
    diagonal = [column_of(states[0][0], m) for m in range(SUB)]
    for j in range(count):
        base = SUB * j
        tiles = [state[j] for state in states]
        has_next = j + 1 < count
        if has_next:
            beside = [column_of(states[0][j + 1], base + m) for m in range(SUB)]
            ahead = [column_of(states[0][j + 1], base + SUB + m) for m in range(SUB)]
        scales, pivot_rows, coefficients, multipliers, growth = [], [], {}, [], [[] for _ in range(SUB)]
        scale_column = None
        for k in range(SUB):
            lower = jnp.where(below[k], diagonal[k], 0.0)
            scale = lax.rsqrt(row_of(diagonal[k], k))
            scales.append(scale)
            rows = [row_of(tile, k) * scale for tile in tiles]
            pivot_rows.append(rows)
            scale_column = scale if k == 0 else jnp.where(sublane == k, scale, scale_column)
            if k + 1 < SUB:
                factor = lower * scale
                for m in range(k + 1, SUB):
                    entry = row_of(diagonal[k], m)
                    coefficients[k, m] = entry * scale
                    if m == k + 1:
                        diagonal[m] = diagonal[m] - (lower * entry) * (scale * scale)
                    else:
                        diagonal[m] = diagonal[m] - factor * coefficients[k, m]
                tiles = [tile - factor * row for tile, row in zip(tiles, rows)]
            if has_next:
                multiplier = beside[k] * scale
                multipliers.append(multiplier)
                for m in range(k + 1, SUB):
                    beside[m] = beside[m] - multiplier * coefficients[k, m]
                for m in range(SUB):
                    growth[m].append(multiplier * row_of(multiplier, m))
        for result, tile in zip(results, tiles):
            result.append(tile * scale_column)
        if has_next:
            diagonal = [ahead[m] - tree_sum(growth[m]) for m in range(SUB)]
            for s, state in enumerate(states):
                state[j + 1] = state[j + 1] - tree_sum([multipliers[k] * pivot_rows[k][s] for k in range(SUB)])
        for i in range(j + 2, count):
            multipliers = []
            for m in range(SUB):
                entry = column_of(states[0][i], base + m)
                for k in range(m):
                    entry = entry - multipliers[k] * coefficients[k, m]
                multipliers.append(entry * scales[m])
            for s, state in enumerate(states):
                state[i] = state[i] - tree_sum([multipliers[k] * pivot_rows[k][s] for k in range(SUB)])
    return [jnp.concatenate(result, 0) for result in results]


def tiles_of(matrix):
    return [matrix[SUB * i:SUB * (i + 1)] for i in range(matrix.shape[0] // SUB)]


def exact(left, right, left_dim, right_dim):
    return lax.dot_general(left, right, (((left_dim,), (right_dim,)), ((), ())), precision=HIGHEST_PREC)


def twice(matrix):
    return jnp.concatenate([matrix, matrix], 0)


def rotation_transposed(gram):
    half = gram.shape[0] // 2
    squared = exact(gram, gram, 1, 0)
    (top,) = sweep(tiles_of(squared[:half]), [])
    change = exact(top[:, half:], top, 0, 0)
    lower_rows = squared[half:] - change
    lower_rows = jnp.concatenate([lower_rows[:, half:], lower_rows[:, half:]], 1)
    (bottom,) = sweep(tiles_of(lower_rows), [])
    bottom = jnp.where(lax.broadcasted_iota(jnp.int32, bottom.shape, 1) >= half, bottom, 0.0)
    first = sweep(tiles_of(exact(top, twice(top), 1, 1)), [tiles_of(top)])[1]
    mixed = exact(bottom, twice(first), 1, 1)
    cross = mixed[:, :half]
    inner = exact(bottom, twice(bottom), 1, 1) - exact(cross, twice(cross), 1, 1)
    second = sweep(tiles_of(inner), [tiles_of(bottom - exact(cross, first, 1, 0))])[1]
    return jnp.concatenate([first, second], 0)


def split(values):
    high = values.astype(jnp.bfloat16)
    return high, (values - high.astype(jnp.float32)).astype(jnp.bfloat16)


def three_pass(left, right, dims):
    left_high, left_low = split(left)
    right_high, right_low = split(right)

    def product(a, b):
        return lax.dot_general(a, b, (dims, ((), ())), preferred_element_type=jnp.float32)

    return product(left_high, right_high) + (product(left_high, right_low) + product(left_low, right_high))


def gram_kernel(columns, gram):
    gram[...] = three_pass(columns[...], columns[...], ((1,), (1,)))


def first_turn_kernel(*refs):
    grams = [ref[...] for ref in refs[:-1]]
    refs[-1][...] = rotation_transposed(tree_sum(grams))


def turn_kernel(entries, stay, moving, turn):
    pair = jnp.concatenate([stay[:, :entries], moving[:, :entries]], 0)
    turn[...] = rotation_transposed(three_pass(pair, pair, ((1,), (1,))))


def rotate_kernel(turn, upper, lower, *outputs):
    pair = jnp.concatenate([upper[...], lower[...]], 0)
    width = upper.shape[0]
    for index, output in enumerate(outputs):
        output[...] = three_pass(turn[width * index:width * (index + 1), :], pair, ((1,), (0,)))


def square_call(kernel, size, *operands):
    return pl.pallas_call(
        kernel, out_shape=jax.ShapeDtypeStruct((size, size), operands[0].dtype), compiler_params=KERNEL_PARAMS
    )(*operands)


def rotate(turn, upper, lower, halves):
    return pl.pallas_call(
        rotate_kernel,
        out_shape=(jax.ShapeDtypeStruct(upper.shape, upper.dtype),) * halves,
        input_output_aliases={1: 0},
        compiler_params=KERNEL_PARAMS,
    )(turn, upper, lower)


def body(columns, right_factor):
    size, own = columns.shape
    width = size // 2
    row_devices = lax.axis_size("rows")
    others = range(1, row_devices)

    def from_near_other(block, distance):
        pairs = lax.axis_size("blk")
        route = [
            (p * row_devices + (r - distance) % row_devices, (p + 1) % pairs * row_devices + r)
            for p in range(pairs) for r in range(row_devices)
        ]
        return lax.ppermute(block, ("blk", "rows"), route)

    near_own = shifted(columns, "blk", 1)
    gram = square_call(gram_kernel, size, columns)
    grams = [gram] + [shifted(gram, "rows", d) for d in others]
    foreign = [shifted(columns, "rows", d) for d in others]
    near_factor = shifted(right_factor, "blk", 1)
    turn = square_call(first_turn_kernel, size, *grams)
    near_foreign = [from_near_other(columns, d) for d in others]
    everywhere = jnp.concatenate([columns, *foreign, right_factor], 1)
    near = jnp.concatenate([near_own, *near_foreign, near_factor], 1)

    def finish(turn, stay, moving, near_stay, near_moving):
        near_turn = shifted(turn, "blk", 1)
        (stay,) = rotate(turn, stay, moving, 1)
        near_stay, moving = rotate(near_turn, near_stay, near_moving, 2)
        return stay, moving, near_stay

    def advance(step_index, state):
        stay, moving, near_stay = state
        near_moving = shifted(moving, "blk", 1)
        turn = square_call(functools.partial(turn_kernel, own * row_devices), size, stay, moving)
        return finish(turn, stay, moving, near_stay, near_moving)

    state = finish(turn, everywhere[:width], everywhere[width:], near[:width], near[width:])
    stay, moving, _ = lax.fori_loop(1, STEPS, advance, state)
    result = jnp.concatenate([stay, moving], 0)
    return result[:, :own], result[:, own * row_devices:]


def solution(mesh):
    return jax.shard_map(
        body,
        mesh=mesh,
        in_specs=(P("blk", "rows"), P("blk", "rows")),
        out_specs=(P("blk", "rows"), P("blk", "rows")),
        check_vma=False,
    )
```

time: 119 us -> 95.9 us (0.81)
  Pallas kernels: 58.7 us -> 37.5 us
  waiting for transfers between devices: 51 us -> 46.6 us
  starting transfers between devices: 5.17 us -> 7 us
  local copies, waits for them, and re-layouts: 1.91 us -> 3.58 us
  other arithmetic: 1.41 us -> 0 us
    pallas_call x18 -> x19, Pallas kernels: 58.7 us -> 37.5 us  [the longest x7 32.5 us: square_call(): pl.pallas_call(kernel, out_shape=jax.ShapeDtypeStruct((size, size), opera...]
    ppermute x21 -> x15, waiting for transfers between devices: 51 us -> 46.6 us  [shifted(): lax.ppermute(block, axis, [((i - distance) % size, i) for i in range(size)])]
    ppermute x0 -> x1, starting transfers between devices: none -> 1.77 us  [from_near_other(): return lax.ppermute(block, ('blk', 'rows'), route)]
    slice x3, local copies, waits for them, and re-layouts: 0.03 us -> 1.47 us  [the longest x2 1.41 us: body(): return (result[:, :own], result[:, own * row_devices:])]
    concatenate x2 -> x0, other arithmetic: 1.41 us -> none  [the longest x1 0.75 us: body(): jnp.concatenate([stay[:, :own], moving[:, :own]], 0)]
    ppermute x21 -> x15, starting transfers between devices: 5.17 us -> 5.23 us  [shifted(): lax.ppermute(block, axis, [((i - distance) % size, i) for i in range(size)])]
  transfers between devices with their start and end apart: 21 -> 16, of which waited for: 14 -> 7; matrix products, arithmetic and copies ran while one was open for 1% -> 0% of each run, Pallas kernels for 47% -> 36%
where the time goes in v3:
time: 95.9 us; the launch traced here: 95.8 us
  waiting for transfers between devices  46.6 us (49%)
  Pallas kernels  37.5 us (39%)
  starting transfers between devices  7 us (7%)
  local copies, waits for them, and re-layouts  3.58 us (4%)
    ppermute x15, waiting for transfers between devices, shifted(): lax.ppermute(block, axis, [((i - distance) % size, i) for i in range(size)])  46.6 us
    pallas_call x7, Pallas kernels, square_call(): pl.pallas_call(kernel, out_shape=jax.ShapeDtypeStruct((size, size), opera...  32.5 us
    ppermute x15, starting transfers between devices, shifted(): lax.ppermute(block, axis, [((i - distance) % size, i) for i in range(size)])  5.23 us
    pallas_call x12, Pallas kernels, rotate(): pl.pallas_call(rotate_kernel, out_shape=(jax.ShapeDtypeStruct(upper.shape...  5.04 us
    unnamed x11, local copies, waits for them, and re-layouts  2.01 us
  transfers between devices with their start and end apart: 16, of which 7 were waited for; matrix products, arithmetic and copies ran while one was open for 0% of the time, Pallas kernels for 36%

profile of v3, /device:TPU:0, one launch (start us, length us, event | category | flops | bytes accessed | tf_op | source)
XLA Modules:
  0.0 95.8 jit_solution(3222078805409390309)
XLA Ops:
  0.6 3.0 %collective-permute-start.3 = (f32[128,640]{1,0:T(8,128)}, f32[128,640]{1,0:T(8,128)S(1)}, u32[]{:S(2)}, u32[]{:S(2)}) collective-permute-start(f32[128,640]{1,0:T(8,128)} %columns.1), channel_id=1, source_target_pairs={{1,0},{0,1},{3,2},{2,3},{5,4},{4,5},{7,6},{6,7},{9,8},{8,9},{11,10... | collective-permute-start | bytes 983048 | tf_op jit(solution)/shard_map/ppermute | solution.py:20
  3.7 1.8 %collective-permute-start.6 = (f32[128,640]{1,0:T(8,128)}, f32[128,640]{1,0:T(8,128)S(1)}, u32[]{:S(2)}, u32[]{:S(2)}) collective-permute-start(f32[128,640]{1,0:T(8,128)} %columns.1), channel_id=1, source_target_pairs={{1,2},{0,3},{3,4},{2,5},{5,6},{4,7},{7,8},{6,9},{9,10},{8,11},{11,... | collective-permute-start | bytes 983048 | tf_op jit(solution)/shard_map/ppermute | solution.py:190
  5.4 1.0 %copy-done = f32[128,640]{1,0:T(8,128)S(1)} copy-done((f32[128,640]{1,0:T(8,128)S(1)}, f32[128,640]{1,0:T(8,128)}, u32[]{:S(2)}) %copy-start) | copy-done | bytes 327704
  6.8 1.6 %collective-permute-start.2 = (f32[128,128]{1,0:T(8,128)S(1)}, f32[128,128]{1,0:T(8,128)S(1)}, u32[]{:S(2)}, u32[]{:S(2)}) collective-permute-start(f32[128,128]{1,0:T(8,128)S(1)} %shard_map.41.refs_0_), channel_id=1, source_target_pairs={{1,0},{0,1},{3,2},{2,3},{5,4},{4,5},{7,6},{6,7},{9,8},{8,9},{11,10... | collective-permute-start | bytes 196616 | tf_op jit(solution)/shard_map/ppermute | solution.py:20
  8.4 0.9 copy-done.2
  9.2 10.8 %collective-permute-done.2.refs_1_ = f32[128,128]{1,0:T(8,128)S(1)} collective-permute-done((f32[128,128]{1,0:T(8,128)S(1)}, f32[128,128]{1,0:T(8,128)S(1)}, u32[]{:S(2)}, u32[]{:S(2)}) %collective-permute-start.2) | collective-permute-done | bytes 65568 | tf_op jit(solution)/shard_map/ppermute | solution.py:20
  20.0 4.8 %shard_map.42.turn = f32[128,128]{1,0:T(8,128)S(1)} custom-call(f32[128,128]{1,0:T(8,128)S(1)} %shard_map.41.refs_0_, f32[128,128]{1,0:T(8,128)S(1)} %collective-permute-done.2.refs_1_), custom_call_target="tpu_custom_call" | custom-call | tf_op jit(solution)/shard_map/pallas_call | solution.py:164
  25.6 5.7 %collective-permute-done.4.turn = f32[128,128]{1,0:T(8,128)S(1)} collective-permute-done((f32[128,128]{1,0:T(8,128)S(1)}, f32[128,128]{1,0:T(8,128)S(1)}, u32[]{:S(2)}, u32[]{:S(2)}) %collective-permute-start.4) | collective-permute-done | bytes 65568 | tf_op jit(solution)/shard_map/ppermute | solution.py:20
  31.3 0.5 shard_map.44
  31.8 62.5 %while.14 = (s32[]{:T(128)}, f32[64,1536]{1,0:T(8,128)S(1)}, f32[64,1536]{1,0:T(8,128)S(1)}, f32[64,1536]{1,0:T(8,128)S(1)}, s32[]{:T(128)}) while((s32[]{:T(128)}, f32[64,1536]{1,0:T(8,128)S(1)}, f32[64,1536]{1,0:T(8,128)S(1)}, f32[64,1536]{1,0:T(8,128)S(1)}, s32[]{:T(128)}) %tuple.24), condition=%wide.region_1.0_spmd, body=%wide.region_0.0_spmd.sunk | while | flops 2 | bytes 1835149 | solution.py:215
  31.9 5.5 %eval_jaxpr.3.turn = f32[128,128]{1,0:T(8,128)S(1)} custom-call(f32[64,1536]{1,0:T(8,128)S(1)} %get-tuple-element.80.stay.upper, f32[64,1536]{1,0:T(8,128)S(1)} %get-tuple-element.81.moving.lower), custom_call_target="tpu_custom_call" | custom-call | tf_op jit(solution)/shard_map/while/body/eval_jaxpr/pallas_call | solution.py:164
  37.8 6.0 %collective-permute-done.turn = f32[128,128]{1,0:T(8,128)S(1)} collective-permute-done((f32[128,128]{1,0:T(8,128)S(1)}, f32[128,128]{1,0:T(8,128)S(1)}, u32[]{:S(2)}, u32[]{:S(2)}) %collective-permute-start) | collective-permute-done | bytes 65568 | tf_op jit(solution)/shard_map/while/body/eval_jaxpr/ppermute | solution.py:20
  43.8 0.5 eval_jaxpr.5
  44.4 5.5 %eval_jaxpr.3.turn = f32[128,128]{1,0:T(8,128)S(1)} custom-call(f32[64,1536]{1,0:T(8,128)S(1)} %get-tuple-element.80.stay.upper, f32[64,1536]{1,0:T(8,128)S(1)} %get-tuple-element.81.moving.lower), custom_call_target="tpu_custom_call" | custom-call | tf_op jit(solution)/shard_map/while/body/eval_jaxpr/pallas_call | solution.py:164
  50.3 6.0 %collective-permute-done.turn = f32[128,128]{1,0:T(8,128)S(1)} collective-permute-done((f32[128,128]{1,0:T(8,128)S(1)}, f32[128,128]{1,0:T(8,128)S(1)}, u32[]{:S(2)}, u32[]{:S(2)}) %collective-permute-start) | collective-permute-done | bytes 65568 | tf_op jit(solution)/shard_map/while/body/eval_jaxpr/ppermute | solution.py:20
  56.3 0.5 eval_jaxpr.5
  56.9 5.5 %eval_jaxpr.3.turn = f32[128,128]{1,0:T(8,128)S(1)} custom-call(f32[64,1536]{1,0:T(8,128)S(1)} %get-tuple-element.80.stay.upper, f32[64,1536]{1,0:T(8,128)S(1)} %get-tuple-element.81.moving.lower), custom_call_target="tpu_custom_call" | custom-call | tf_op jit(solution)/shard_map/while/body/eval_jaxpr/pallas_call | solution.py:164
  62.8 6.0 %collective-permute-done.turn = f32[128,128]{1,0:T(8,128)S(1)} collective-permute-done((f32[128,128]{1,0:T(8,128)S(1)}, f32[128,128]{1,0:T(8,128)S(1)}, u32[]{:S(2)}, u32[]{:S(2)}) %collective-permute-start) | collective-permute-done | bytes 65568 | tf_op jit(solution)/shard_map/while/body/eval_jaxpr/ppermute | solution.py:20
  69.4 5.5 %eval_jaxpr.3.turn = f32[128,128]{1,0:T(8,128)S(1)} custom-call(f32[64,1536]{1,0:T(8,128)S(1)} %get-tuple-element.80.stay.upper, f32[64,1536]{1,0:T(8,128)S(1)} %get-tuple-element.81.moving.lower), custom_call_target="tpu_custom_call" | custom-call | tf_op jit(solution)/shard_map/while/body/eval_jaxpr/pallas_call | solution.py:164
  75.3 6.0 %collective-permute-done.turn = f32[128,128]{1,0:T(8,128)S(1)} collective-permute-done((f32[128,128]{1,0:T(8,128)S(1)}, f32[128,128]{1,0:T(8,128)S(1)}, u32[]{:S(2)}, u32[]{:S(2)}) %collective-permute-start) | collective-permute-done | bytes 65568 | tf_op jit(solution)/shard_map/while/body/eval_jaxpr/ppermute | solution.py:20
  81.9 5.5 %eval_jaxpr.3.turn = f32[128,128]{1,0:T(8,128)S(1)} custom-call(f32[64,1536]{1,0:T(8,128)S(1)} %get-tuple-element.80.stay.upper, f32[64,1536]{1,0:T(8,128)S(1)} %get-tuple-element.81.moving.lower), custom_call_target="tpu_custom_call" | custom-call | tf_op jit(solution)/shard_map/while/body/eval_jaxpr/pallas_call | solution.py:164
  87.8 6.0 %collective-permute-done.turn = f32[128,128]{1,0:T(8,128)S(1)} collective-permute-done((f32[128,128]{1,0:T(8,128)S(1)}, f32[128,128]{1,0:T(8,128)S(1)}, u32[]{:S(2)}, u32[]{:S(2)}) %collective-permute-start) | collective-permute-done | bytes 65568 | tf_op jit(solution)/shard_map/while/body/eval_jaxpr/ppermute | solution.py:20
  94.4 0.8 slice.28
  95.1 0.7 slice.29
  (46 shorter events, 4.9 us)
Async XLA Ops:
  0.6 24.3 %collective-permute-start.3 = (f32[128,640]{1,0:T(8,128)}, f32[128,640]{1,0:T(8,128)S(1)}, u32[]{:S(2)}, u32[]{:S(2)}) collective-permute-start(f32[128,640]{1,0:T(8,128)} %columns.1), channel_id=1, source_target_pairs={{1,0},{0,1},{3,2},{2,3},{5,4},{4,5},{7,6},{6,7},{9,8},{8,9},{11,10... | collective-permute-start | bytes 983048 | tf_op jit(solution)/shard_map/ppermute | solution.py:20
  3.7 21.4 %collective-permute-start.5 = (f32[128,640]{1,0:T(8,128)}, f32[128,640]{1,0:T(8,128)S(1)}, u32[]{:S(2)}, u32[]{:S(2)}) collective-permute-start(f32[128,640]{1,0:T(8,128)} %columns.1), channel_id=1, source_target_pairs={{30,0},{0,2},{2,4},{4,6},{6,8},{8,10},{10,12},{12,14},{14,16},{16,... | collective-permute-start | bytes 983048 | tf_op jit(solution)/shard_map/ppermute | solution.py:20
  3.7 21.4 %collective-permute-start.6 = (f32[128,640]{1,0:T(8,128)}, f32[128,640]{1,0:T(8,128)S(1)}, u32[]{:S(2)}, u32[]{:S(2)}) collective-permute-start(f32[128,640]{1,0:T(8,128)} %columns.1), channel_id=1, source_target_pairs={{1,2},{0,3},{3,4},{2,5},{5,6},{4,7},{7,8},{6,9},{9,10},{8,11},{11,... | collective-permute-start | bytes 983048 | tf_op jit(solution)/shard_map/ppermute | solution.py:190
  5.4 1.0 %copy-start = (f32[128,640]{1,0:T(8,128)S(1)}, f32[128,640]{1,0:T(8,128)}, u32[]{:S(2)}) copy-start(f32[128,640]{1,0:T(8,128)} %columns.1) | copy-start | bytes 983044
  6.4 1.9 %copy-start.1 = (f32[128,640]{1,0:T(8,128)S(1)}, f32[128,640]{1,0:T(8,128)}, u32[]{:S(2)}) copy-start(f32[128,640]{1,0:T(8,128)} %columns.1) | copy-start | bytes 983044
  6.8 13.2 %collective-permute-start.2 = (f32[128,128]{1,0:T(8,128)S(1)}, f32[128,128]{1,0:T(8,128)S(1)}, u32[]{:S(2)}, u32[]{:S(2)}) collective-permute-start(f32[128,128]{1,0:T(8,128)S(1)} %shard_map.41.refs_0_), channel_id=1, source_target_pairs={{1,0},{0,1},{3,2},{2,3},{5,4},{4,5},{7,6},{6,7},{9,8},{8,9},{11,10... | collective-permute-start | bytes 196616 | tf_op jit(solution)/shard_map/ppermute | solution.py:20
  8.3 0.9 copy-start.2
  9.2 15.9 %collective-permute-start.7 = (f32[128,256]{1,0:T(8,128)S(1)}, f32[128,256]{1,0:T(8,128)S(1)}, u32[]{:S(2)}, u32[]{:S(2)}) collective-permute-start(f32[128,256]{1,0:T(8,128)S(1)} %copy-done.2), channel_id=1, source_target_pairs={{30,0},{0,2},{2,4},{4,6},{6,8},{8,10},{10,12},{12,14},{14,16},{16,... | collective-permute-start | bytes 393224 | tf_op jit(solution)/shard_map/ppermute | solution.py:20
  24.8 6.4 %collective-permute-start.4 = (f32[128,128]{1,0:T(8,128)S(1)}, f32[128,128]{1,0:T(8,128)S(1)}, u32[]{:S(2)}, u32[]{:S(2)}) collective-permute-start(f32[128,128]{1,0:T(8,128)S(1)} %shard_map.42.turn), channel_id=1, source_target_pairs={{30,0},{0,2},{2,4},{4,6},{6,8},{8,10},{10,12},{12,14},{14,16},{16,... | collective-permute-start | bytes 196616 | tf_op jit(solution)/shard_map/ppermute | solution.py:20
  31.8 12.0 %collective-permute-start.1 = (f32[64,1536]{1,0:T(8,128)S(1)}, f32[64,1536]{1,0:T(8,128)S(1)}, u32[]{:S(2)}, u32[]{:S(2)}) collective-permute-start(f32[64,1536]{1,0:T(8,128)S(1)} %get-tuple-element.81.moving.lower), channel_id=1, source_target_pairs={{30,0},{0,2},{2,4},{4,6},{6,8},{8,10},{10,12},{12,14},{14,16},{16,... | collective-permute-start | bytes 1179656 | tf_op jit(solution)/shard_map/while/body/eval_jaxpr/ppermute | solution.py:20
  37.3 6.4 %collective-permute-start = (f32[128,128]{1,0:T(8,128)S(1)}, f32[128,128]{1,0:T(8,128)S(1)}, u32[]{:S(2)}, u32[]{:S(2)}) collective-permute-start(f32[128,128]{1,0:T(8,128)S(1)} %eval_jaxpr.3.turn), channel_id=1, source_target_pairs={{30,0},{0,2},{2,4},{4,6},{6,8},{8,10},{10,12},{12,14},{14,16},{16,... | collective-permute-start | bytes 196616 | tf_op jit(solution)/shard_map/while/body/eval_jaxpr/ppermute | solution.py:20
  44.3 12.0 %collective-permute-start.1 = (f32[64,1536]{1,0:T(8,128)S(1)}, f32[64,1536]{1,0:T(8,128)S(1)}, u32[]{:S(2)}, u32[]{:S(2)}) collective-permute-start(f32[64,1536]{1,0:T(8,128)S(1)} %get-tuple-element.81.moving.lower), channel_id=1, source_target_pairs={{30,0},{0,2},{2,4},{4,6},{6,8},{8,10},{10,12},{12,14},{14,16},{16,... | collective-permute-start | bytes 1179656 | tf_op jit(solution)/shard_map/while/body/eval_jaxpr/ppermute | solution.py:20
  49.8 6.4 %collective-permute-start = (f32[128,128]{1,0:T(8,128)S(1)}, f32[128,128]{1,0:T(8,128)S(1)}, u32[]{:S(2)}, u32[]{:S(2)}) collective-permute-start(f32[128,128]{1,0:T(8,128)S(1)} %eval_jaxpr.3.turn), channel_id=1, source_target_pairs={{30,0},{0,2},{2,4},{4,6},{6,8},{8,10},{10,12},{12,14},{14,16},{16,... | collective-permute-start | bytes 196616 | tf_op jit(solution)/shard_map/while/body/eval_jaxpr/ppermute | solution.py:20
  56.8 12.0 %collective-permute-start.1 = (f32[64,1536]{1,0:T(8,128)S(1)}, f32[64,1536]{1,0:T(8,128)S(1)}, u32[]{:S(2)}, u32[]{:S(2)}) collective-permute-start(f32[64,1536]{1,0:T(8,128)S(1)} %get-tuple-element.81.moving.lower), channel_id=1, source_target_pairs={{30,0},{0,2},{2,4},{4,6},{6,8},{8,10},{10,12},{12,14},{14,16},{16,... | collective-permute-start | bytes 1179656 | tf_op jit(solution)/shard_map/while/body/eval_jaxpr/ppermute | solution.py:20
  62.3 6.4 %collective-permute-start = (f32[128,128]{1,0:T(8,128)S(1)}, f32[128,128]{1,0:T(8,128)S(1)}, u32[]{:S(2)}, u32[]{:S(2)}) collective-permute-start(f32[128,128]{1,0:T(8,128)S(1)} %eval_jaxpr.3.turn), channel_id=1, source_target_pairs={{30,0},{0,2},{2,4},{4,6},{6,8},{8,10},{10,12},{12,14},{14,16},{16,... | collective-permute-start | bytes 196616 | tf_op jit(solution)/shard_map/while/body/eval_jaxpr/ppermute | solution.py:20
  69.3 12.0 %collective-permute-start.1 = (f32[64,1536]{1,0:T(8,128)S(1)}, f32[64,1536]{1,0:T(8,128)S(1)}, u32[]{:S(2)}, u32[]{:S(2)}) collective-permute-start(f32[64,1536]{1,0:T(8,128)S(1)} %get-tuple-element.81.moving.lower), channel_id=1, source_target_pairs={{30,0},{0,2},{2,4},{4,6},{6,8},{8,10},{10,12},{12,14},{14,16},{16,... | collective-permute-start | bytes 1179656 | tf_op jit(solution)/shard_map/while/body/eval_jaxpr/ppermute | solution.py:20
  74.8 6.4 %collective-permute-start = (f32[128,128]{1,0:T(8,128)S(1)}, f32[128,128]{1,0:T(8,128)S(1)}, u32[]{:S(2)}, u32[]{:S(2)}) collective-permute-start(f32[128,128]{1,0:T(8,128)S(1)} %eval_jaxpr.3.turn), channel_id=1, source_target_pairs={{30,0},{0,2},{2,4},{4,6},{6,8},{8,10},{10,12},{12,14},{14,16},{16,... | collective-permute-start | bytes 196616 | tf_op jit(solution)/shard_map/while/body/eval_jaxpr/ppermute | solution.py:20
  81.8 12.0 %collective-permute-start.1 = (f32[64,1536]{1,0:T(8,128)S(1)}, f32[64,1536]{1,0:T(8,128)S(1)}, u32[]{:S(2)}, u32[]{:S(2)}) collective-permute-start(f32[64,1536]{1,0:T(8,128)S(1)} %get-tuple-element.81.moving.lower), channel_id=1, source_target_pairs={{30,0},{0,2},{2,4},{4,6},{6,8},{8,10},{10,12},{12,14},{14,16},{16,... | collective-permute-start | bytes 1179656 | tf_op jit(solution)/shard_map/while/body/eval_jaxpr/ppermute | solution.py:20
  87.3 6.4 %collective-permute-start = (f32[128,128]{1,0:T(8,128)S(1)}, f32[128,128]{1,0:T(8,128)S(1)}, u32[]{:S(2)}, u32[]{:S(2)}) collective-permute-start(f32[128,128]{1,0:T(8,128)S(1)} %eval_jaxpr.3.turn), channel_id=1, source_target_pairs={{30,0},{0,2},{2,4},{4,6},{6,8},{8,10},{10,12},{12,14},{14,16},{16,... | collective-permute-start | bytes 196616 | tf_op jit(solution)/shard_map/while/body/eval_jaxpr/ppermute | solution.py:20

commit v4 on v3

--- a/solution.py
+++ b/solution.py
@@ -54,21 +54,21 @@
         scales, pivot_rows, coefficients, multipliers, growth = [], [], {}, [], [[] for _ in range(SUB)]
         scale_column = None
         for k in range(SUB):
+            pivot = row_of(diagonal[0], 0) if k == 0 else next_pivot
             lower = jnp.where(below[k], diagonal[k], 0.0)
-            scale = lax.rsqrt(row_of(diagonal[k], k))
+            scale = lax.rsqrt(pivot)
             scales.append(scale)
+            if k + 1 < SUB:
+                entry = row_of(diagonal[k], k + 1)
+                next_pivot = row_of(diagonal[k + 1], k + 1) - (entry * entry) * (scale * scale)
             rows = [row_of(tile, k) * scale for tile in tiles]
             pivot_rows.append(rows)
             scale_column = scale if k == 0 else jnp.where(sublane == k, scale, scale_column)
             if k + 1 < SUB:
                 factor = lower * scale
                 for m in range(k + 1, SUB):
-                    entry = row_of(diagonal[k], m)
-                    coefficients[k, m] = entry * scale
-                    if m == k + 1:
-                        diagonal[m] = diagonal[m] - (lower * entry) * (scale * scale)
-                    else:
-                        diagonal[m] = diagonal[m] - factor * coefficients[k, m]
+                    coefficients[k, m] = row_of(diagonal[k], m) * scale
+                    diagonal[m] = diagonal[m] - factor * coefficients[k, m]
                 tiles = [tile - factor * row for tile, row in zip(tiles, rows)]
             if has_next:
                 multiplier = beside[k] * scale
@@ -111,16 +111,15 @@
     half = gram.shape[0] // 2
     squared = exact(gram, gram, 1, 0)
     (top,) = sweep(tiles_of(squared[:half]), [])
-    change = exact(top[:, half:], top, 0, 0)
+    change = three_pass(top[:, half:], top, ((0,), (0,)))
     lower_rows = squared[half:] - change
     lower_rows = jnp.concatenate([lower_rows[:, half:], lower_rows[:, half:]], 1)
     (bottom,) = sweep(tiles_of(lower_rows), [])
     bottom = jnp.where(lax.broadcasted_iota(jnp.int32, bottom.shape, 1) >= half, bottom, 0.0)
     first = sweep(tiles_of(exact(top, twice(top), 1, 1)), [tiles_of(top)])[1]
-    mixed = exact(bottom, twice(first), 1, 1)
-    cross = mixed[:, :half]
-    inner = exact(bottom, twice(bottom), 1, 1) - exact(cross, twice(cross), 1, 1)
-    second = sweep(tiles_of(inner), [tiles_of(bottom - exact(cross, first, 1, 0))])[1]
+    cross = three_pass(bottom, first, ((1,), (1,)))
+    inner = exact(bottom, twice(bottom), 1, 1) - three_pass(cross, twice(cross), ((1,), (1,)))
+    second = sweep(tiles_of(inner), [tiles_of(bottom - three_pass(cross, first, ((1,), (0,))))])[1]
     return jnp.concatenate([first, second], 0)
 
 
@@ -160,6 +159,36 @@
         output[...] = three_pass(turn[width * index:width * (index + 1), :], pair, ((1,), (0,)))
 
 
+def rotate_pieces_kernel(halves, turn, *refs):
+    pieces, outputs = refs[:-halves], refs[-halves:]
+    width = turn.shape[0] // 2
+    start = 0
+    for piece in pieces:
+        stop = start + piece.shape[1]
+        for index, output in enumerate(outputs):
+            rows = turn[width * index:width * (index + 1), :]
+            output[:, start:stop] = three_pass(rows, piece[...], ((1,), (0,)))
+        start = stop
+
+
+def deliver_kernel(stay, moving, new_columns, new_factor, sems):
+    width = stay.shape[0]
+    own = new_columns.shape[1]
+    factor_at = stay.shape[1] - new_factor.shape[1]
+    copies = []
+    for index, block in enumerate((stay, moving)):
+        rows = pl.ds(width * index, width)
+        copies.append((block.at[:, pl.ds(0, own)], new_columns.at[rows, :]))
+        copies.append((block.at[:, pl.ds(factor_at, new_factor.shape[1])], new_factor.at[rows, :]))
+    started = [
+        pltpu.make_async_copy(source, target, sems.at[n]) for n, (source, target) in enumerate(copies)
+    ]
+    for copy in started:
+        copy.start()
+    for copy in started:
+        copy.wait()
+
+
 def square_call(kernel, size, *operands):
     return pl.pallas_call(
         kernel, out_shape=jax.ShapeDtypeStruct((size, size), operands[0].dtype), compiler_params=KERNEL_PARAMS
@@ -175,9 +204,31 @@
     )(turn, upper, lower)
 
 
+def rotate_pieces(turn, pieces, halves):
+    width = turn.shape[0] // 2
+    total = sum(piece.shape[1] for piece in pieces)
+    return pl.pallas_call(
+        functools.partial(rotate_pieces_kernel, halves),
+        out_shape=(jax.ShapeDtypeStruct((width, total), turn.dtype),) * halves,
+        compiler_params=KERNEL_PARAMS,
+    )(turn, *pieces)
+
+
+def deliver(stay, moving, own, factor_rows):
+    size = 2 * stay.shape[0]
+    return pl.pallas_call(
+        deliver_kernel,
+        out_shape=tuple(jax.ShapeDtypeStruct((size, n), stay.dtype) for n in (own, factor_rows)),
+        in_specs=[pl.BlockSpec(memory_space=pltpu.VMEM)] * 2,
+        out_specs=(pl.BlockSpec(memory_space=pl.ANY),) * 2,
+        scratch_shapes=(pltpu.SemaphoreType.DMA((4,)),),
+        compiler_params=KERNEL_PARAMS,
+        name="deliver",
+    )(stay, moving)
+
+
 def body(columns, right_factor):
     size, own = columns.shape
-    width = size // 2
     row_devices = lax.axis_size("rows")
     others = range(1, row_devices)
 
@@ -196,8 +247,6 @@
     near_factor = shifted(right_factor, "blk", 1)
     turn = square_call(first_turn_kernel, size, *grams)
     near_foreign = [from_near_other(columns, d) for d in others]
-    everywhere = jnp.concatenate([columns, *foreign, right_factor], 1)
-    near = jnp.concatenate([near_own, *near_foreign, near_factor], 1)
 
     def finish(turn, stay, moving, near_stay, near_moving):
         near_turn = shifted(turn, "blk", 1)
@@ -211,10 +260,11 @@
         turn = square_call(functools.partial(turn_kernel, own * row_devices), size, stay, moving)
         return finish(turn, stay, moving, near_stay, near_moving)
 
-    state = finish(turn, everywhere[:width], everywhere[width:], near[:width], near[width:])
-    stay, moving, _ = lax.fori_loop(1, STEPS, advance, state)
-    result = jnp.concatenate([stay, moving], 0)
-    return result[:, :own], result[:, own * row_devices:]
+    near_turn = shifted(turn, "blk", 1)
+    (stay,) = rotate_pieces(turn, (columns, *foreign, right_factor), 1)
+    near_stay, moving = rotate_pieces(near_turn, (near_own, *near_foreign, near_factor), 2)
+    stay, moving, _ = lax.fori_loop(1, STEPS, advance, (stay, moving, near_stay))
+    return deliver(stay, moving, own, right_factor.shape[1])
 
 
 def solution(mesh):

time: 95.9 us -> 94.3 us (0.983)
  local copies, waits for them, and re-layouts: 3.58 us -> 0.98 us
  waiting for transfers between devices: 46.6 us -> 47.9 us
    ppermute x1, starting transfers between devices: 1.77 us -> 0.01 us  [from_near_other(): return lax.ppermute(block, ('blk', 'rows'), route)]
    pallas_call x0 -> x3, Pallas kernels: none -> 1.75 us  [the longest x2 0.95 us: rotate_pieces(): pl.pallas_call(functools.partial(rotate_pieces_kernel, halves), out_shape...]
    ppermute x15, starting transfers between devices: 5.23 us -> 6.83 us  [shifted(): lax.ppermute(block, axis, [((i - distance) % size, i) for i in range(size)])]
    slice x4 -> x0, local copies, waits for them, and re-layouts: 1.52 us -> none  [the longest x2 1.41 us: body(): return (result[:, :own], result[:, own * row_devices:])]
    ppermute x15, waiting for transfers between devices: 46.6 us -> 47.9 us  [shifted(): lax.ppermute(block, axis, [((i - distance) % size, i) for i in range(size)])]
    unnamed x11 -> x6, local copies, waits for them, and re-layouts: 2.01 us -> 0.98 us
    pallas_call x7, Pallas kernels: 32.5 us -> 31.5 us  [square_call(): pl.pallas_call(kernel, out_shape=jax.ShapeDtypeStruct((size, size), opera...]
    pallas_call x12 -> x10, Pallas kernels: 5.04 us -> 4.2 us  [rotate(): pl.pallas_call(rotate_kernel, out_shape=(jax.ShapeDtypeStruct(upper.shape...]
where the time goes in v4:
time: 94.3 us; the launch traced here: 94.2 us
  waiting for transfers between devices  47.9 us (51%)
  Pallas kernels  37.4 us (40%)
  starting transfers between devices  6.83 us (7%)
  local copies, waits for them, and re-layouts  0.98 us (1%)
    ppermute x15, waiting for transfers between devices, shifted(): lax.ppermute(block, axis, [((i - distance) % size, i) for i in range(size)])  47.9 us
    pallas_call x7, Pallas kernels, square_call(): pl.pallas_call(kernel, out_shape=jax.ShapeDtypeStruct((size, size), opera...  31.5 us
    ppermute x15, starting transfers between devices, shifted(): lax.ppermute(block, axis, [((i - distance) % size, i) for i in range(size)])  6.83 us
    pallas_call x10, Pallas kernels, rotate(): pl.pallas_call(rotate_kernel, out_shape=(jax.ShapeDtypeStruct(upper.shape...  4.2 us
  transfers between devices with their start and end apart: 16, of which 7 were waited for; matrix products, arithmetic and copies ran while one was open for 0% of the time, Pallas kernels for 36%

profile of v4, /device:TPU:0, one launch (start us, length us, event | category | flops | bytes accessed | tf_op | source)
XLA Modules:
  0.0 94.2 jit_solution(7960165977286830898)
XLA Ops:
  0.6 3.0 %collective-permute-start.3 = (f32[128,640]{1,0:T(8,128)}, f32[128,640]{1,0:T(8,128)S(1)}, u32[]{:S(2)}, u32[]{:S(2)}) collective-permute-start(f32[128,640]{1,0:T(8,128)} %refs_0_.1), channel_id=1, source_target_pairs={{1,0},{0,1},{3,2},{2,3},{5,4},{4,5},{7,6},{6,7},{9,8},{8,9},{11,10... | collective-permute-start | bytes 983048 | tf_op jit(solution)/shard_map/ppermute | solution.py:20
  3.7 1.6 %collective-permute-start.5 = (f32[128,640]{1,0:T(8,128)}, f32[128,640]{1,0:T(8,128)S(1)}, u32[]{:S(2)}, u32[]{:S(2)}) collective-permute-start(f32[128,640]{1,0:T(8,128)} %refs_0_.1), channel_id=1, source_target_pairs={{30,0},{0,2},{2,4},{4,6},{6,8},{8,10},{10,12},{12,14},{14,16},{16,... | collective-permute-start | bytes 983048 | tf_op jit(solution)/shard_map/ppermute | solution.py:20
  5.3 1.0 %copy-done = f32[128,640]{1,0:T(8,128)S(1)} copy-done((f32[128,640]{1,0:T(8,128)S(1)}, f32[128,640]{1,0:T(8,128)}, u32[]{:S(2)}) %copy-start) | copy-done | bytes 327704
  6.6 1.6 %collective-permute-start.2 = (f32[128,128]{1,0:T(8,128)S(1)}, f32[128,128]{1,0:T(8,128)S(1)}, u32[]{:S(2)}, u32[]{:S(2)}) collective-permute-start(f32[128,128]{1,0:T(8,128)S(1)} %shard_map.41.refs_0_), channel_id=1, source_target_pairs={{1,0},{0,1},{3,2},{2,3},{5,4},{4,5},{7,6},{6,7},{9,8},{8,9},{11,10... | collective-permute-start | bytes 196616 | tf_op jit(solution)/shard_map/ppermute | solution.py:20
  8.1 11.9 %collective-permute-done.2.refs_1_ = f32[128,128]{1,0:T(8,128)S(1)} collective-permute-done((f32[128,128]{1,0:T(8,128)S(1)}, f32[128,128]{1,0:T(8,128)S(1)}, u32[]{:S(2)}, u32[]{:S(2)}) %collective-permute-start.2) | collective-permute-done | bytes 65568 | tf_op jit(solution)/shard_map/ppermute | solution.py:20
  20.0 4.6 %shard_map.42.turn = f32[128,128]{1,0:T(8,128)S(1)} custom-call(f32[128,128]{1,0:T(8,128)S(1)} %shard_map.41.refs_0_, f32[128,128]{1,0:T(8,128)S(1)} %collective-permute-done.2.refs_1_), custom_call_target="tpu_custom_call" | custom-call | tf_op jit(solution)/shard_map/pallas_call | solution.py:193
  25.1 6.0 %collective-permute-done.4.turn = f32[128,128]{1,0:T(8,128)S(1)} collective-permute-done((f32[128,128]{1,0:T(8,128)S(1)}, f32[128,128]{1,0:T(8,128)S(1)}, u32[]{:S(2)}, u32[]{:S(2)}) %collective-permute-start.4) | collective-permute-done | bytes 65568 | tf_op jit(solution)/shard_map/ppermute | solution.py:20
  31.1 0.6 shard_map.44
  31.7 61.7 %while.14 = (s32[]{:T(128)}, f32[64,1536]{1,0:T(8,128)S(1)}, f32[64,1536]{1,0:T(8,128)S(1)}, f32[64,1536]{1,0:T(8,128)S(1)}, s32[]{:T(128)}) while((s32[]{:T(128)}, f32[64,1536]{1,0:T(8,128)S(1)}, f32[64,1536]{1,0:T(8,128)S(1)}, f32[64,1536]{1,0:T(8,128)S(1)}, s32[]{:T(128)}) %tuple.20), condition=%wide.region_1.0_spmd, body=%wide.region_0.0_spmd.sunk | while | flops 2 | bytes 1835149 | solution.py:266
  31.8 5.3 %eval_jaxpr.3.turn = f32[128,128]{1,0:T(8,128)S(1)} custom-call(f32[64,1536]{1,0:T(8,128)S(1)} %get-tuple-element.76.stay.upper, f32[64,1536]{1,0:T(8,128)S(1)} %get-tuple-element.77.moving.lower), custom_call_target="tpu_custom_call" | custom-call | tf_op jit(solution)/shard_map/while/body/eval_jaxpr/pallas_call | solution.py:193
  37.5 6.0 %collective-permute-done.turn = f32[128,128]{1,0:T(8,128)S(1)} collective-permute-done((f32[128,128]{1,0:T(8,128)S(1)}, f32[128,128]{1,0:T(8,128)S(1)}, u32[]{:S(2)}, u32[]{:S(2)}) %collective-permute-start) | collective-permute-done | bytes 65568 | tf_op jit(solution)/shard_map/while/body/eval_jaxpr/ppermute | solution.py:20
  43.5 0.5 eval_jaxpr.5
  44.1 5.3 %eval_jaxpr.3.turn = f32[128,128]{1,0:T(8,128)S(1)} custom-call(f32[64,1536]{1,0:T(8,128)S(1)} %get-tuple-element.76.stay.upper, f32[64,1536]{1,0:T(8,128)S(1)} %get-tuple-element.77.moving.lower), custom_call_target="tpu_custom_call" | custom-call | tf_op jit(solution)/shard_map/while/body/eval_jaxpr/pallas_call | solution.py:193
  49.9 6.0 %collective-permute-done.turn = f32[128,128]{1,0:T(8,128)S(1)} collective-permute-done((f32[128,128]{1,0:T(8,128)S(1)}, f32[128,128]{1,0:T(8,128)S(1)}, u32[]{:S(2)}, u32[]{:S(2)}) %collective-permute-start) | collective-permute-done | bytes 65568 | tf_op jit(solution)/shard_map/while/body/eval_jaxpr/ppermute | solution.py:20
  55.9 0.5 eval_jaxpr.5
  56.4 5.3 %eval_jaxpr.3.turn = f32[128,128]{1,0:T(8,128)S(1)} custom-call(f32[64,1536]{1,0:T(8,128)S(1)} %get-tuple-element.76.stay.upper, f32[64,1536]{1,0:T(8,128)S(1)} %get-tuple-element.77.moving.lower), custom_call_target="tpu_custom_call" | custom-call | tf_op jit(solution)/shard_map/while/body/eval_jaxpr/pallas_call | solution.py:193
  62.2 6.0 %collective-permute-done.turn = f32[128,128]{1,0:T(8,128)S(1)} collective-permute-done((f32[128,128]{1,0:T(8,128)S(1)}, f32[128,128]{1,0:T(8,128)S(1)}, u32[]{:S(2)}, u32[]{:S(2)}) %collective-permute-start) | collective-permute-done | bytes 65568 | tf_op jit(solution)/shard_map/while/body/eval_jaxpr/ppermute | solution.py:20
  68.2 0.5 eval_jaxpr.5
  68.8 5.3 %eval_jaxpr.3.turn = f32[128,128]{1,0:T(8,128)S(1)} custom-call(f32[64,1536]{1,0:T(8,128)S(1)} %get-tuple-element.76.stay.upper, f32[64,1536]{1,0:T(8,128)S(1)} %get-tuple-element.77.moving.lower), custom_call_target="tpu_custom_call" | custom-call | tf_op jit(solution)/shard_map/while/body/eval_jaxpr/pallas_call | solution.py:193
  74.5 6.0 %collective-permute-done.turn = f32[128,128]{1,0:T(8,128)S(1)} collective-permute-done((f32[128,128]{1,0:T(8,128)S(1)}, f32[128,128]{1,0:T(8,128)S(1)}, u32[]{:S(2)}, u32[]{:S(2)}) %collective-permute-start) | collective-permute-done | bytes 65568 | tf_op jit(solution)/shard_map/while/body/eval_jaxpr/ppermute | solution.py:20
  80.5 0.5 eval_jaxpr.5
  81.1 5.3 %eval_jaxpr.3.turn = f32[128,128]{1,0:T(8,128)S(1)} custom-call(f32[64,1536]{1,0:T(8,128)S(1)} %get-tuple-element.76.stay.upper, f32[64,1536]{1,0:T(8,128)S(1)} %get-tuple-element.77.moving.lower), custom_call_target="tpu_custom_call" | custom-call | tf_op jit(solution)/shard_map/while/body/eval_jaxpr/pallas_call | solution.py:193
  86.9 6.0 %collective-permute-done.turn = f32[128,128]{1,0:T(8,128)S(1)} collective-permute-done((f32[128,128]{1,0:T(8,128)S(1)}, f32[128,128]{1,0:T(8,128)S(1)}, u32[]{:S(2)}, u32[]{:S(2)}) %collective-permute-start) | collective-permute-done | bytes 65568 | tf_op jit(solution)/shard_map/while/body/eval_jaxpr/ppermute | solution.py:20
  93.4 0.8 deliver.1
  (35 shorter events, 3.6 us)
Async XLA Ops:
  0.6 24.1 %collective-permute-start.3 = (f32[128,640]{1,0:T(8,128)}, f32[128,640]{1,0:T(8,128)S(1)}, u32[]{:S(2)}, u32[]{:S(2)}) collective-permute-start(f32[128,640]{1,0:T(8,128)} %refs_0_.1), channel_id=1, source_target_pairs={{1,0},{0,1},{3,2},{2,3},{5,4},{4,5},{7,6},{6,7},{9,8},{8,9},{11,10... | collective-permute-start | bytes 983048 | tf_op jit(solution)/shard_map/ppermute | solution.py:20
  3.7 27.4 %collective-permute-start.6 = (f32[128,640]{1,0:T(8,128)}, f32[128,640]{1,0:T(8,128)S(1)}, u32[]{:S(2)}, u32[]{:S(2)}) collective-permute-start(f32[128,640]{1,0:T(8,128)} %refs_0_.1), channel_id=1, source_target_pairs={{1,2},{0,3},{3,4},{2,5},{5,6},{4,7},{7,8},{6,9},{9,10},{8,11},{11,... | collective-permute-start | bytes 983048 | tf_op jit(solution)/shard_map/ppermute | solution.py:241
  3.7 27.4 %collective-permute-start.5 = (f32[128,640]{1,0:T(8,128)}, f32[128,640]{1,0:T(8,128)S(1)}, u32[]{:S(2)}, u32[]{:S(2)}) collective-permute-start(f32[128,640]{1,0:T(8,128)} %refs_0_.1), channel_id=1, source_target_pairs={{30,0},{0,2},{2,4},{4,6},{6,8},{8,10},{10,12},{12,14},{14,16},{16,... | collective-permute-start | bytes 983048 | tf_op jit(solution)/shard_map/ppermute | solution.py:20
  5.3 1.0 %copy-start = (f32[128,640]{1,0:T(8,128)S(1)}, f32[128,640]{1,0:T(8,128)}, u32[]{:S(2)}) copy-start(f32[128,640]{1,0:T(8,128)} %refs_0_.1) | copy-start | bytes 983044
  6.2 18.5 %copy-start.1 = (f32[128,640]{1,0:T(8,128)S(1)}, f32[128,640]{1,0:T(8,128)}, u32[]{:S(2)}) copy-start(f32[128,640]{1,0:T(8,128)} %refs_0_.1) | copy-start | bytes 983044
  6.6 18.2 %copy-start.2 = (f32[128,256]{1,0:T(8,128)S(1)}, f32[128,256]{1,0:T(8,128)}, u32[]{:S(2)}) copy-start(f32[128,256]{1,0:T(8,128)} %refs_2_.1) | copy-start | bytes 393220
  6.6 13.4 %collective-permute-start.2 = (f32[128,128]{1,0:T(8,128)S(1)}, f32[128,128]{1,0:T(8,128)S(1)}, u32[]{:S(2)}, u32[]{:S(2)}) collective-permute-start(f32[128,128]{1,0:T(8,128)S(1)} %shard_map.41.refs_0_), channel_id=1, source_target_pairs={{1,0},{0,1},{3,2},{2,3},{5,4},{4,5},{7,6},{6,7},{9,8},{8,9},{11,10... | collective-permute-start | bytes 196616 | tf_op jit(solution)/shard_map/ppermute | solution.py:20
  8.1 23.0 %collective-permute-start.7 = (f32[128,256]{1,0:T(8,128)}, f32[128,256]{1,0:T(8,128)S(1)}, u32[]{:S(2)}, u32[]{:S(2)}) collective-permute-start(f32[128,256]{1,0:T(8,128)} %refs_2_.1), channel_id=1, source_target_pairs={{30,0},{0,2},{2,4},{4,6},{6,8},{8,10},{10,12},{12,14},{14,16},{16,... | collective-permute-start | bytes 393224 | tf_op jit(solution)/shard_map/ppermute | solution.py:20
  24.7 6.4 %collective-permute-start.4 = (f32[128,128]{1,0:T(8,128)S(1)}, f32[128,128]{1,0:T(8,128)S(1)}, u32[]{:S(2)}, u32[]{:S(2)}) collective-permute-start(f32[128,128]{1,0:T(8,128)S(1)} %shard_map.42.turn), channel_id=1, source_target_pairs={{30,0},{0,2},{2,4},{4,6},{6,8},{8,10},{10,12},{12,14},{14,16},{16,... | collective-permute-start | bytes 196616 | tf_op jit(solution)/shard_map/ppermute | solution.py:20
  31.7 11.8 %collective-permute-start.1 = (f32[64,1536]{1,0:T(8,128)S(1)}, f32[64,1536]{1,0:T(8,128)S(1)}, u32[]{:S(2)}, u32[]{:S(2)}) collective-permute-start(f32[64,1536]{1,0:T(8,128)S(1)} %get-tuple-element.77.moving.lower), channel_id=1, source_target_pairs={{30,0},{0,2},{2,4},{4,6},{6,8},{8,10},{10,12},{12,14},{14,16},{16,... | collective-permute-start | bytes 1179656 | tf_op jit(solution)/shard_map/while/body/eval_jaxpr/ppermute | solution.py:20
  37.1 6.4 %collective-permute-start = (f32[128,128]{1,0:T(8,128)S(1)}, f32[128,128]{1,0:T(8,128)S(1)}, u32[]{:S(2)}, u32[]{:S(2)}) collective-permute-start(f32[128,128]{1,0:T(8,128)S(1)} %eval_jaxpr.3.turn), channel_id=1, source_target_pairs={{30,0},{0,2},{2,4},{4,6},{6,8},{8,10},{10,12},{12,14},{14,16},{16,... | collective-permute-start | bytes 196616 | tf_op jit(solution)/shard_map/while/body/eval_jaxpr/ppermute | solution.py:20
  44.0 11.8 %collective-permute-start.1 = (f32[64,1536]{1,0:T(8,128)S(1)}, f32[64,1536]{1,0:T(8,128)S(1)}, u32[]{:S(2)}, u32[]{:S(2)}) collective-permute-start(f32[64,1536]{1,0:T(8,128)S(1)} %get-tuple-element.77.moving.lower), channel_id=1, source_target_pairs={{30,0},{0,2},{2,4},{4,6},{6,8},{8,10},{10,12},{12,14},{14,16},{16,... | collective-permute-start | bytes 1179656 | tf_op jit(solution)/shard_map/while/body/eval_jaxpr/ppermute | solution.py:20
  49.4 6.4 %collective-permute-start = (f32[128,128]{1,0:T(8,128)S(1)}, f32[128,128]{1,0:T(8,128)S(1)}, u32[]{:S(2)}, u32[]{:S(2)}) collective-permute-start(f32[128,128]{1,0:T(8,128)S(1)} %eval_jaxpr.3.turn), channel_id=1, source_target_pairs={{30,0},{0,2},{2,4},{4,6},{6,8},{8,10},{10,12},{12,14},{14,16},{16,... | collective-permute-start | bytes 196616 | tf_op jit(solution)/shard_map/while/body/eval_jaxpr/ppermute | solution.py:20
  56.4 11.8 %collective-permute-start.1 = (f32[64,1536]{1,0:T(8,128)S(1)}, f32[64,1536]{1,0:T(8,128)S(1)}, u32[]{:S(2)}, u32[]{:S(2)}) collective-permute-start(f32[64,1536]{1,0:T(8,128)S(1)} %get-tuple-element.77.moving.lower), channel_id=1, source_target_pairs={{30,0},{0,2},{2,4},{4,6},{6,8},{8,10},{10,12},{12,14},{14,16},{16,... | collective-permute-start | bytes 1179656 | tf_op jit(solution)/shard_map/while/body/eval_jaxpr/ppermute | solution.py:20
  61.8 6.4 %collective-permute-start = (f32[128,128]{1,0:T(8,128)S(1)}, f32[128,128]{1,0:T(8,128)S(1)}, u32[]{:S(2)}, u32[]{:S(2)}) collective-permute-start(f32[128,128]{1,0:T(8,128)S(1)} %eval_jaxpr.3.turn), channel_id=1, source_target_pairs={{30,0},{0,2},{2,4},{4,6},{6,8},{8,10},{10,12},{12,14},{14,16},{16,... | collective-permute-start | bytes 196616 | tf_op jit(solution)/shard_map/while/body/eval_jaxpr/ppermute | solution.py:20
  68.7 11.8 %collective-permute-start.1 = (f32[64,1536]{1,0:T(8,128)S(1)}, f32[64,1536]{1,0:T(8,128)S(1)}, u32[]{:S(2)}, u32[]{:S(2)}) collective-permute-start(f32[64,1536]{1,0:T(8,128)S(1)} %get-tuple-element.77.moving.lower), channel_id=1, source_target_pairs={{30,0},{0,2},{2,4},{4,6},{6,8},{8,10},{10,12},{12,14},{14,16},{16,... | collective-permute-start | bytes 1179656 | tf_op jit(solution)/shard_map/while/body/eval_jaxpr/ppermute | solution.py:20
  74.1 6.4 %collective-permute-start = (f32[128,128]{1,0:T(8,128)S(1)}, f32[128,128]{1,0:T(8,128)S(1)}, u32[]{:S(2)}, u32[]{:S(2)}) collective-permute-start(f32[128,128]{1,0:T(8,128)S(1)} %eval_jaxpr.3.turn), channel_id=1, source_target_pairs={{30,0},{0,2},{2,4},{4,6},{6,8},{8,10},{10,12},{12,14},{14,16},{16,... | collective-permute-start | bytes 196616 | tf_op jit(solution)/shard_map/while/body/eval_jaxpr/ppermute | solution.py:20
  81.1 11.8 %collective-permute-start.1 = (f32[64,1536]{1,0:T(8,128)S(1)}, f32[64,1536]{1,0:T(8,128)S(1)}, u32[]{:S(2)}, u32[]{:S(2)}) collective-permute-start(f32[64,1536]{1,0:T(8,128)S(1)} %get-tuple-element.77.moving.lower), channel_id=1, source_target_pairs={{30,0},{0,2},{2,4},{4,6},{6,8},{8,10},{10,12},{12,14},{14,16},{16,... | collective-permute-start | bytes 1179656 | tf_op jit(solution)/shard_map/while/body/eval_jaxpr/ppermute | solution.py:20
  86.4 6.4 %collective-permute-start = (f32[128,128]{1,0:T(8,128)S(1)}, f32[128,128]{1,0:T(8,128)S(1)}, u32[]{:S(2)}, u32[]{:S(2)}) collective-permute-start(f32[128,128]{1,0:T(8,128)S(1)} %eval_jaxpr.3.turn), channel_id=1, source_target_pairs={{30,0},{0,2},{2,4},{4,6},{6,8},{8,10},{10,12},{12,14},{14,16},{16,... | collective-permute-start | bytes 196616 | tf_op jit(solution)/shard_map/while/body/eval_jaxpr/ppermute | solution.py:20

commit v5 on v4

--- a/solution.py
+++ b/solution.py
@@ -10,6 +10,7 @@
 
 STEPS = 6
 SUB = 8
+LATE = 2
 KERNEL_PARAMS = pltpu.CompilerParams(vmem_limit_bytes=24 * 1024 * 1024)
 
 HIGHEST_PREC = lax.Precision.HIGHEST
@@ -50,7 +51,7 @@
         has_next = j + 1 < count
         if has_next:
             beside = [column_of(states[0][j + 1], base + m) for m in range(SUB)]
-            ahead = [column_of(states[0][j + 1], base + SUB + m) for m in range(SUB)]
+            ahead = [column_of(states[0][j + 1], base + SUB + m) for m in range(SUB - LATE)]
         scales, pivot_rows, coefficients, multipliers, growth = [], [], {}, [], [[] for _ in range(SUB)]
         scale_column = None
         for k in range(SUB):
@@ -75,14 +76,15 @@
                 multipliers.append(multiplier)
                 for m in range(k + 1, SUB):
                     beside[m] = beside[m] - multiplier * coefficients[k, m]
-                for m in range(SUB):
+                for m in range(SUB - LATE):
                     growth[m].append(multiplier * row_of(multiplier, m))
         for result, tile in zip(results, tiles):
             result.append(tile * scale_column)
         if has_next:
-            diagonal = [ahead[m] - tree_sum(growth[m]) for m in range(SUB)]
+            diagonal = [ahead[m] - tree_sum(growth[m]) for m in range(SUB - LATE)]
             for s, state in enumerate(states):
                 state[j + 1] = state[j + 1] - tree_sum([multipliers[k] * pivot_rows[k][s] for k in range(SUB)])
+            diagonal += [column_of(states[0][j + 1], base + SUB + m) for m in range(SUB - LATE, SUB)]
         for i in range(j + 2, count):
             multipliers = []
             for m in range(SUB):
@@ -99,6 +101,28 @@
     return [matrix[SUB * i:SUB * (i + 1)] for i in range(matrix.shape[0] // SUB)]
 
 
+def parts_of(values, count):
+    parts = []
+    for _ in range(count - 1):
+        parts.append(values.astype(jnp.bfloat16))
+        values = values - parts[-1].astype(jnp.float32)
+    return parts + [values.astype(jnp.bfloat16)]
+
+
+def stacked(left, right, left_dim, right_dim, terms):
+    count = 1 + max(max(term) for term in terms)
+    lefts, rights = parts_of(left, count), parts_of(right, count)
+    return lax.dot_general(
+        jnp.concatenate([lefts[a] for a, _ in terms], left_dim),
+        jnp.concatenate([rights[b] for _, b in terms], right_dim),
+        (((left_dim,), (right_dim,)), ((), ())),
+        preferred_element_type=jnp.float32,
+    )
+
+
+THREE_TERMS = ((0, 1), (1, 0), (0, 0))
+
+
 def exact(left, right, left_dim, right_dim):
     return lax.dot_general(left, right, (((left_dim,), (right_dim,)), ((), ())), precision=HIGHEST_PREC)
 
@@ -111,13 +135,13 @@
     half = gram.shape[0] // 2
     squared = exact(gram, gram, 1, 0)
     (top,) = sweep(tiles_of(squared[:half]), [])
-    change = three_pass(top[:, half:], top, ((0,), (0,)))
-    lower_rows = squared[half:] - change
+    change = stacked(top, top, 0, 0, THREE_TERMS)
+    lower_rows = squared[half:] - change[half:]
     lower_rows = jnp.concatenate([lower_rows[:, half:], lower_rows[:, half:]], 1)
     (bottom,) = sweep(tiles_of(lower_rows), [])
     bottom = jnp.where(lax.broadcasted_iota(jnp.int32, bottom.shape, 1) >= half, bottom, 0.0)
     first = sweep(tiles_of(exact(top, twice(top), 1, 1)), [tiles_of(top)])[1]
-    cross = three_pass(bottom, first, ((1,), (1,)))
+    cross = stacked(bottom, first, 1, 1, THREE_TERMS)
     inner = exact(bottom, twice(bottom), 1, 1) - three_pass(cross, twice(cross), ((1,), (1,)))
     second = sweep(tiles_of(inner), [tiles_of(bottom - three_pass(cross, first, ((1,), (0,))))])[1]
     return jnp.concatenate([first, second], 0)
@@ -138,8 +162,17 @@
     return product(left_high, right_high) + (product(left_high, right_low) + product(left_low, right_high))
 
 
+def gram_of(pair):
+    high, low = split(pair)
+    size = pair.shape[0]
+    both = lax.dot_general(
+        jnp.concatenate([low, high], 0), high, (((1,), (1,)), ((), ())), preferred_element_type=jnp.float32
+    )
+    return both[size:] + (both[:size] + both[:size].T)
+
+
 def gram_kernel(columns, gram):
-    gram[...] = three_pass(columns[...], columns[...], ((1,), (1,)))
+    gram[...] = gram_of(columns[...])
 
 
 def first_turn_kernel(*refs):
@@ -149,14 +182,26 @@
 
 def turn_kernel(entries, stay, moving, turn):
     pair = jnp.concatenate([stay[:, :entries], moving[:, :entries]], 0)
-    turn[...] = rotation_transposed(three_pass(pair, pair, ((1,), (1,))))
+    turn[...] = rotation_transposed(gram_of(pair))
+
+
+def turned(rows, values):
+    rows_high, rows_low = split(rows)
+    high, low = split(values)
+
+    def product(a, b):
+        return jnp.dot(a, b, preferred_element_type=jnp.float32)
+
+    both = product(jnp.concatenate([rows_high, rows_high], 1), jnp.concatenate([high, low], 0))
+    return both + product(rows_low, high)
 
 
 def rotate_kernel(turn, upper, lower, *outputs):
     pair = jnp.concatenate([upper[...], lower[...]], 0)
     width = upper.shape[0]
+    rotated = turned(turn[:width * len(outputs), :], pair)
     for index, output in enumerate(outputs):
-        output[...] = three_pass(turn[width * index:width * (index + 1), :], pair, ((1,), (0,)))
+        output[...] = rotated[width * index:width * (index + 1)]
 
 
 def rotate_pieces_kernel(halves, turn, *refs):

time: 94.3 us -> 92.1 us (0.977)
  Pallas kernels: 37.4 us -> 35.1 us
    pallas_call x7, Pallas kernels: 31.5 us -> 29.9 us  [square_call(): pl.pallas_call(kernel, out_shape=jax.ShapeDtypeStruct((size, size), opera...]
  transfers between devices with their start and end apart: 16 -> 16, of which waited for: 7 -> 7; matrix products, arithmetic and copies ran while one was open for 0% -> 0% of each run, Pallas kernels for 36% -> 35%
where the time goes in v5:
time: 92.1 us; the launch traced here: 91.9 us
  waiting for transfers between devices  48.1 us (52%)
  Pallas kernels  35.1 us (38%)
  starting transfers between devices  6.83 us (7%)
  local copies, waits for them, and re-layouts  0.98 us (1%)
    ppermute x15, waiting for transfers between devices, shifted(): lax.ppermute(block, axis, [((i - distance) % size, i) for i in range(size)])  48.1 us
    pallas_call x7, Pallas kernels, square_call(): pl.pallas_call(kernel, out_shape=jax.ShapeDtypeStruct((size, size), opera...  29.9 us
    ppermute x15, starting transfers between devices, shifted(): lax.ppermute(block, axis, [((i - distance) % size, i) for i in range(size)])  6.83 us
    pallas_call x10, Pallas kernels, rotate(): pl.pallas_call(rotate_kernel, out_shape=(jax.ShapeDtypeStruct(upper.shape...  3.37 us
  transfers between devices with their start and end apart: 16, of which 7 were waited for; matrix products, arithmetic and copies ran while one was open for 0% of the time, Pallas kernels for 35%

profile of v5, /device:TPU:0, one launch (start us, length us, event | category | flops | bytes accessed | tf_op | source)
XLA Modules:
  0.0 91.9 jit_solution(1397449853845534494)
XLA Ops:
  0.6 3.0 %collective-permute-start.3 = (f32[128,640]{1,0:T(8,128)}, f32[128,640]{1,0:T(8,128)S(1)}, u32[]{:S(2)}, u32[]{:S(2)}) collective-permute-start(f32[128,640]{1,0:T(8,128)} %refs_0_.1), channel_id=1, source_target_pairs={{1,0},{0,1},{3,2},{2,3},{5,4},{4,5},{7,6},{6,7},{9,8},{8,9},{11,10... | collective-permute-start | bytes 983048 | tf_op jit(solution)/shard_map/ppermute | solution.py:21
  3.7 1.6 %collective-permute-start.5 = (f32[128,640]{1,0:T(8,128)}, f32[128,640]{1,0:T(8,128)S(1)}, u32[]{:S(2)}, u32[]{:S(2)}) collective-permute-start(f32[128,640]{1,0:T(8,128)} %refs_0_.1), channel_id=1, source_target_pairs={{30,0},{0,2},{2,4},{4,6},{6,8},{8,10},{10,12},{12,14},{14,16},{16,... | collective-permute-start | bytes 983048 | tf_op jit(solution)/shard_map/ppermute | solution.py:21
  5.3 1.0 %copy-done = f32[128,640]{1,0:T(8,128)S(1)} copy-done((f32[128,640]{1,0:T(8,128)S(1)}, f32[128,640]{1,0:T(8,128)}, u32[]{:S(2)}) %copy-start) | copy-done | bytes 327704
  6.6 1.6 %collective-permute-start.2 = (f32[128,128]{1,0:T(8,128)S(1)}, f32[128,128]{1,0:T(8,128)S(1)}, u32[]{:S(2)}, u32[]{:S(2)}) collective-permute-start(f32[128,128]{1,0:T(8,128)S(1)} %shard_map.41.refs_0_), channel_id=1, source_target_pairs={{1,0},{0,1},{3,2},{2,3},{5,4},{4,5},{7,6},{6,7},{9,8},{8,9},{11,10... | collective-permute-start | bytes 196616 | tf_op jit(solution)/shard_map/ppermute | solution.py:21
  8.2 11.9 %collective-permute-done.2.refs_1_ = f32[128,128]{1,0:T(8,128)S(1)} collective-permute-done((f32[128,128]{1,0:T(8,128)S(1)}, f32[128,128]{1,0:T(8,128)S(1)}, u32[]{:S(2)}, u32[]{:S(2)}) %collective-permute-start.2) | collective-permute-done | bytes 65568 | tf_op jit(solution)/shard_map/ppermute | solution.py:21
  20.0 4.5 %shard_map.42.turn = f32[128,128]{1,0:T(8,128)S(1)} custom-call(f32[128,128]{1,0:T(8,128)S(1)} %shard_map.41.refs_0_, f32[128,128]{1,0:T(8,128)S(1)} %collective-permute-done.2.refs_1_), custom_call_target="tpu_custom_call" | custom-call | tf_op jit(solution)/shard_map/pallas_call | solution.py:238
  24.6 0.4 shard_map.43
  25.0 6.0 %collective-permute-done.4.turn = f32[128,128]{1,0:T(8,128)S(1)} collective-permute-done((f32[128,128]{1,0:T(8,128)S(1)}, f32[128,128]{1,0:T(8,128)S(1)}, u32[]{:S(2)}, u32[]{:S(2)}) %collective-permute-start.4) | collective-permute-done | bytes 65568 | tf_op jit(solution)/shard_map/ppermute | solution.py:21
  31.0 0.6 shard_map.44
  31.5 59.6 %while.14 = (s32[]{:T(128)}, f32[64,1536]{1,0:T(8,128)S(1)}, f32[64,1536]{1,0:T(8,128)S(1)}, f32[64,1536]{1,0:T(8,128)S(1)}, s32[]{:T(128)}) while((s32[]{:T(128)}, f32[64,1536]{1,0:T(8,128)S(1)}, f32[64,1536]{1,0:T(8,128)S(1)}, f32[64,1536]{1,0:T(8,128)S(1)}, s32[]{:T(128)}) %tuple.20), condition=%wide.region_1.0_spmd, body=%wide.region_0.0_spmd.sunk | while | flops 2 | bytes 1835149 | solution.py:311
  31.6 5.0 %eval_jaxpr.3.turn = f32[128,128]{1,0:T(8,128)S(1)} custom-call(f32[64,1536]{1,0:T(8,128)S(1)} %get-tuple-element.76.stay.upper, f32[64,1536]{1,0:T(8,128)S(1)} %get-tuple-element.77.moving.lower), custom_call_target="tpu_custom_call" | custom-call | tf_op jit(solution)/shard_map/while/body/eval_jaxpr/pallas_call | solution.py:238
  37.1 6.0 %collective-permute-done.turn = f32[128,128]{1,0:T(8,128)S(1)} collective-permute-done((f32[128,128]{1,0:T(8,128)S(1)}, f32[128,128]{1,0:T(8,128)S(1)}, u32[]{:S(2)}, u32[]{:S(2)}) %collective-permute-start) | collective-permute-done | bytes 65568 | tf_op jit(solution)/shard_map/while/body/eval_jaxpr/ppermute | solution.py:21
  43.5 5.0 %eval_jaxpr.3.turn = f32[128,128]{1,0:T(8,128)S(1)} custom-call(f32[64,1536]{1,0:T(8,128)S(1)} %get-tuple-element.76.stay.upper, f32[64,1536]{1,0:T(8,128)S(1)} %get-tuple-element.77.moving.lower), custom_call_target="tpu_custom_call" | custom-call | tf_op jit(solution)/shard_map/while/body/eval_jaxpr/pallas_call | solution.py:238
  49.0 6.0 %collective-permute-done.turn = f32[128,128]{1,0:T(8,128)S(1)} collective-permute-done((f32[128,128]{1,0:T(8,128)S(1)}, f32[128,128]{1,0:T(8,128)S(1)}, u32[]{:S(2)}, u32[]{:S(2)}) %collective-permute-start) | collective-permute-done | bytes 65568 | tf_op jit(solution)/shard_map/while/body/eval_jaxpr/ppermute | solution.py:21
  55.0 0.3 eval_jaxpr.5
  55.4 5.0 %eval_jaxpr.3.turn = f32[128,128]{1,0:T(8,128)S(1)} custom-call(f32[64,1536]{1,0:T(8,128)S(1)} %get-tuple-element.76.stay.upper, f32[64,1536]{1,0:T(8,128)S(1)} %get-tuple-element.77.moving.lower), custom_call_target="tpu_custom_call" | custom-call | tf_op jit(solution)/shard_map/while/body/eval_jaxpr/pallas_call | solution.py:238
  60.9 6.0 %collective-permute-done.turn = f32[128,128]{1,0:T(8,128)S(1)} collective-permute-done((f32[128,128]{1,0:T(8,128)S(1)}, f32[128,128]{1,0:T(8,128)S(1)}, u32[]{:S(2)}, u32[]{:S(2)}) %collective-permute-start) | collective-permute-done | bytes 65568 | tf_op jit(solution)/shard_map/while/body/eval_jaxpr/ppermute | solution.py:21
  66.9 0.3 eval_jaxpr.5
  67.4 5.0 %eval_jaxpr.3.turn = f32[128,128]{1,0:T(8,128)S(1)} custom-call(f32[64,1536]{1,0:T(8,128)S(1)} %get-tuple-element.76.stay.upper, f32[64,1536]{1,0:T(8,128)S(1)} %get-tuple-element.77.moving.lower), custom_call_target="tpu_custom_call" | custom-call | tf_op jit(solution)/shard_map/while/body/eval_jaxpr/pallas_call | solution.py:238
  72.8 6.0 %collective-permute-done.turn = f32[128,128]{1,0:T(8,128)S(1)} collective-permute-done((f32[128,128]{1,0:T(8,128)S(1)}, f32[128,128]{1,0:T(8,128)S(1)}, u32[]{:S(2)}, u32[]{:S(2)}) %collective-permute-start) | collective-permute-done | bytes 65568 | tf_op jit(solution)/shard_map/while/body/eval_jaxpr/ppermute | solution.py:21
  79.3 5.0 %eval_jaxpr.3.turn = f32[128,128]{1,0:T(8,128)S(1)} custom-call(f32[64,1536]{1,0:T(8,128)S(1)} %get-tuple-element.76.stay.upper, f32[64,1536]{1,0:T(8,128)S(1)} %get-tuple-element.77.moving.lower), custom_call_target="tpu_custom_call" | custom-call | tf_op jit(solution)/shard_map/while/body/eval_jaxpr/pallas_call | solution.py:238
  84.7 6.0 %collective-permute-done.turn = f32[128,128]{1,0:T(8,128)S(1)} collective-permute-done((f32[128,128]{1,0:T(8,128)S(1)}, f32[128,128]{1,0:T(8,128)S(1)}, u32[]{:S(2)}, u32[]{:S(2)}) %collective-permute-start) | collective-permute-done | bytes 65568 | tf_op jit(solution)/shard_map/while/body/eval_jaxpr/ppermute | solution.py:21
  90.7 0.3 eval_jaxpr.5
  91.1 0.8 deliver.1
  (35 shorter events, 3.3 us)
Async XLA Ops:
  0.6 23.9 %collective-permute-start.3 = (f32[128,640]{1,0:T(8,128)}, f32[128,640]{1,0:T(8,128)S(1)}, u32[]{:S(2)}, u32[]{:S(2)}) collective-permute-start(f32[128,640]{1,0:T(8,128)} %refs_0_.1), channel_id=1, source_target_pairs={{1,0},{0,1},{3,2},{2,3},{5,4},{4,5},{7,6},{6,7},{9,8},{8,9},{11,10... | collective-permute-start | bytes 983048 | tf_op jit(solution)/shard_map/ppermute | solution.py:21
  3.7 27.3 %collective-permute-start.6 = (f32[128,640]{1,0:T(8,128)}, f32[128,640]{1,0:T(8,128)S(1)}, u32[]{:S(2)}, u32[]{:S(2)}) collective-permute-start(f32[128,640]{1,0:T(8,128)} %refs_0_.1), channel_id=1, source_target_pairs={{1,2},{0,3},{3,4},{2,5},{5,6},{4,7},{7,8},{6,9},{9,10},{8,11},{11,... | collective-permute-start | bytes 983048 | tf_op jit(solution)/shard_map/ppermute | solution.py:286
  3.7 27.3 %collective-permute-start.5 = (f32[128,640]{1,0:T(8,128)}, f32[128,640]{1,0:T(8,128)S(1)}, u32[]{:S(2)}, u32[]{:S(2)}) collective-permute-start(f32[128,640]{1,0:T(8,128)} %refs_0_.1), channel_id=1, source_target_pairs={{30,0},{0,2},{2,4},{4,6},{6,8},{8,10},{10,12},{12,14},{14,16},{16,... | collective-permute-start | bytes 983048 | tf_op jit(solution)/shard_map/ppermute | solution.py:21
  5.3 1.0 %copy-start = (f32[128,640]{1,0:T(8,128)S(1)}, f32[128,640]{1,0:T(8,128)}, u32[]{:S(2)}) copy-start(f32[128,640]{1,0:T(8,128)} %refs_0_.1) | copy-start | bytes 983044
  6.2 18.3 %copy-start.1 = (f32[128,640]{1,0:T(8,128)S(1)}, f32[128,640]{1,0:T(8,128)}, u32[]{:S(2)}) copy-start(f32[128,640]{1,0:T(8,128)} %refs_0_.1) | copy-start | bytes 983044
  6.6 18.0 %copy-start.2 = (f32[128,256]{1,0:T(8,128)S(1)}, f32[128,256]{1,0:T(8,128)}, u32[]{:S(2)}) copy-start(f32[128,256]{1,0:T(8,128)} %refs_2_.1) | copy-start | bytes 393220
  6.6 13.4 %collective-permute-start.2 = (f32[128,128]{1,0:T(8,128)S(1)}, f32[128,128]{1,0:T(8,128)S(1)}, u32[]{:S(2)}, u32[]{:S(2)}) collective-permute-start(f32[128,128]{1,0:T(8,128)S(1)} %shard_map.41.refs_0_), channel_id=1, source_target_pairs={{1,0},{0,1},{3,2},{2,3},{5,4},{4,5},{7,6},{6,7},{9,8},{8,9},{11,10... | collective-permute-start | bytes 196616 | tf_op jit(solution)/shard_map/ppermute | solution.py:21
  8.1 22.8 %collective-permute-start.7 = (f32[128,256]{1,0:T(8,128)}, f32[128,256]{1,0:T(8,128)S(1)}, u32[]{:S(2)}, u32[]{:S(2)}) collective-permute-start(f32[128,256]{1,0:T(8,128)} %refs_2_.1), channel_id=1, source_target_pairs={{30,0},{0,2},{2,4},{4,6},{6,8},{8,10},{10,12},{12,14},{14,16},{16,... | collective-permute-start | bytes 393224 | tf_op jit(solution)/shard_map/ppermute | solution.py:21
  24.5 6.4 %collective-permute-start.4 = (f32[128,128]{1,0:T(8,128)S(1)}, f32[128,128]{1,0:T(8,128)S(1)}, u32[]{:S(2)}, u32[]{:S(2)}) collective-permute-start(f32[128,128]{1,0:T(8,128)S(1)} %shard_map.42.turn), channel_id=1, source_target_pairs={{30,0},{0,2},{2,4},{4,6},{6,8},{8,10},{10,12},{12,14},{14,16},{16,... | collective-permute-start | bytes 196616 | tf_op jit(solution)/shard_map/ppermute | solution.py:21
  31.6 11.5 %collective-permute-start.1 = (f32[64,1536]{1,0:T(8,128)S(1)}, f32[64,1536]{1,0:T(8,128)S(1)}, u32[]{:S(2)}, u32[]{:S(2)}) collective-permute-start(f32[64,1536]{1,0:T(8,128)S(1)} %get-tuple-element.77.moving.lower), channel_id=1, source_target_pairs={{30,0},{0,2},{2,4},{4,6},{6,8},{8,10},{10,12},{12,14},{14,16},{16,... | collective-permute-start | bytes 1179656 | tf_op jit(solution)/shard_map/while/body/eval_jaxpr/ppermute | solution.py:21
  36.7 6.4 %collective-permute-start = (f32[128,128]{1,0:T(8,128)S(1)}, f32[128,128]{1,0:T(8,128)S(1)}, u32[]{:S(2)}, u32[]{:S(2)}) collective-permute-start(f32[128,128]{1,0:T(8,128)S(1)} %eval_jaxpr.3.turn), channel_id=1, source_target_pairs={{30,0},{0,2},{2,4},{4,6},{6,8},{8,10},{10,12},{12,14},{14,16},{16,... | collective-permute-start | bytes 196616 | tf_op jit(solution)/shard_map/while/body/eval_jaxpr/ppermute | solution.py:21
  43.5 11.5 %collective-permute-start.1 = (f32[64,1536]{1,0:T(8,128)S(1)}, f32[64,1536]{1,0:T(8,128)S(1)}, u32[]{:S(2)}, u32[]{:S(2)}) collective-permute-start(f32[64,1536]{1,0:T(8,128)S(1)} %get-tuple-element.77.moving.lower), channel_id=1, source_target_pairs={{30,0},{0,2},{2,4},{4,6},{6,8},{8,10},{10,12},{12,14},{14,16},{16,... | collective-permute-start | bytes 1179656 | tf_op jit(solution)/shard_map/while/body/eval_jaxpr/ppermute | solution.py:21
  48.6 6.4 %collective-permute-start = (f32[128,128]{1,0:T(8,128)S(1)}, f32[128,128]{1,0:T(8,128)S(1)}, u32[]{:S(2)}, u32[]{:S(2)}) collective-permute-start(f32[128,128]{1,0:T(8,128)S(1)} %eval_jaxpr.3.turn), channel_id=1, source_target_pairs={{30,0},{0,2},{2,4},{4,6},{6,8},{8,10},{10,12},{12,14},{14,16},{16,... | collective-permute-start | bytes 196616 | tf_op jit(solution)/shard_map/while/body/eval_jaxpr/ppermute | solution.py:21
  55.4 11.5 %collective-permute-start.1 = (f32[64,1536]{1,0:T(8,128)S(1)}, f32[64,1536]{1,0:T(8,128)S(1)}, u32[]{:S(2)}, u32[]{:S(2)}) collective-permute-start(f32[64,1536]{1,0:T(8,128)S(1)} %get-tuple-element.77.moving.lower), channel_id=1, source_target_pairs={{30,0},{0,2},{2,4},{4,6},{6,8},{8,10},{10,12},{12,14},{14,16},{16,... | collective-permute-start | bytes 1179656 | tf_op jit(solution)/shard_map/while/body/eval_jaxpr/ppermute | solution.py:21
  60.5 6.4 %collective-permute-start = (f32[128,128]{1,0:T(8,128)S(1)}, f32[128,128]{1,0:T(8,128)S(1)}, u32[]{:S(2)}, u32[]{:S(2)}) collective-permute-start(f32[128,128]{1,0:T(8,128)S(1)} %eval_jaxpr.3.turn), channel_id=1, source_target_pairs={{30,0},{0,2},{2,4},{4,6},{6,8},{8,10},{10,12},{12,14},{14,16},{16,... | collective-permute-start | bytes 196616 | tf_op jit(solution)/shard_map/while/body/eval_jaxpr/ppermute | solution.py:21
  67.3 11.5 %collective-permute-start.1 = (f32[64,1536]{1,0:T(8,128)S(1)}, f32[64,1536]{1,0:T(8,128)S(1)}, u32[]{:S(2)}, u32[]{:S(2)}) collective-permute-start(f32[64,1536]{1,0:T(8,128)S(1)} %get-tuple-element.77.moving.lower), channel_id=1, source_target_pairs={{30,0},{0,2},{2,4},{4,6},{6,8},{8,10},{10,12},{12,14},{14,16},{16,... | collective-permute-start | bytes 1179656 | tf_op jit(solution)/shard_map/while/body/eval_jaxpr/ppermute | solution.py:21
  72.4 6.4 %collective-permute-start = (f32[128,128]{1,0:T(8,128)S(1)}, f32[128,128]{1,0:T(8,128)S(1)}, u32[]{:S(2)}, u32[]{:S(2)}) collective-permute-start(f32[128,128]{1,0:T(8,128)S(1)} %eval_jaxpr.3.turn), channel_id=1, source_target_pairs={{30,0},{0,2},{2,4},{4,6},{6,8},{8,10},{10,12},{12,14},{14,16},{16,... | collective-permute-start | bytes 196616 | tf_op jit(solution)/shard_map/while/body/eval_jaxpr/ppermute | solution.py:21
  79.2 11.5 %collective-permute-start.1 = (f32[64,1536]{1,0:T(8,128)S(1)}, f32[64,1536]{1,0:T(8,128)S(1)}, u32[]{:S(2)}, u32[]{:S(2)}) collective-permute-start(f32[64,1536]{1,0:T(8,128)S(1)} %get-tuple-element.77.moving.lower), channel_id=1, source_target_pairs={{30,0},{0,2},{2,4},{4,6},{6,8},{8,10},{10,12},{12,14},{14,16},{16,... | collective-permute-start | bytes 1179656 | tf_op jit(solution)/shard_map/while/body/eval_jaxpr/ppermute | solution.py:21
  84.3 6.4 %collective-permute-start = (f32[128,128]{1,0:T(8,128)S(1)}, f32[128,128]{1,0:T(8,128)S(1)}, u32[]{:S(2)}, u32[]{:S(2)}) collective-permute-start(f32[128,128]{1,0:T(8,128)S(1)} %eval_jaxpr.3.turn), channel_id=1, source_target_pairs={{30,0},{0,2},{2,4},{4,6},{6,8},{8,10},{10,12},{12,14},{14,16},{16,... | collective-permute-start | bytes 196616 | tf_op jit(solution)/shard_map/while/body/eval_jaxpr/ppermute | solution.py:21

commit v6 on v5

--- a/solution.py
+++ b/solution.py
@@ -120,7 +120,7 @@
     )
 
 
-THREE_TERMS = ((0, 1), (1, 0), (0, 0))
+SIX_TERMS = ((0, 2), (2, 0), (1, 1), (0, 1), (1, 0), (0, 0))
 
 
 def exact(left, right, left_dim, right_dim):
@@ -135,31 +135,21 @@
     half = gram.shape[0] // 2
     squared = exact(gram, gram, 1, 0)
     (top,) = sweep(tiles_of(squared[:half]), [])
-    change = stacked(top, top, 0, 0, THREE_TERMS)
+    change = stacked(top, top, 0, 0, SIX_TERMS)
     lower_rows = squared[half:] - change[half:]
     lower_rows = jnp.concatenate([lower_rows[:, half:], lower_rows[:, half:]], 1)
     (bottom,) = sweep(tiles_of(lower_rows), [])
     bottom = jnp.where(lax.broadcasted_iota(jnp.int32, bottom.shape, 1) >= half, bottom, 0.0)
     first = sweep(tiles_of(exact(top, twice(top), 1, 1)), [tiles_of(top)])[1]
-    cross = stacked(bottom, first, 1, 1, THREE_TERMS)
-    inner = exact(bottom, twice(bottom), 1, 1) - three_pass(cross, twice(cross), ((1,), (1,)))
-    second = sweep(tiles_of(inner), [tiles_of(bottom - three_pass(cross, first, ((1,), (0,))))])[1]
+    cross = stacked(bottom, first, 1, 1, SIX_TERMS)
+    inner = exact(bottom, twice(bottom), 1, 1) - exact(cross, twice(cross), 1, 1)
+    second = sweep(tiles_of(inner), [tiles_of(bottom - exact(cross, first, 1, 0))])[1]
     return jnp.concatenate([first, second], 0)
 
 
 def split(values):
     high = values.astype(jnp.bfloat16)
     return high, (values - high.astype(jnp.float32)).astype(jnp.bfloat16)
-
-
-def three_pass(left, right, dims):
-    left_high, left_low = split(left)
-    right_high, right_low = split(right)
-
-    def product(a, b):
-        return lax.dot_general(a, b, (dims, ((), ())), preferred_element_type=jnp.float32)
-
-    return product(left_high, right_high) + (product(left_high, right_low) + product(left_low, right_high))
 
 
 def gram_of(pair):
@@ -186,14 +176,7 @@
 
 
 def turned(rows, values):
-    rows_high, rows_low = split(rows)
-    high, low = split(values)
-
-    def product(a, b):
-        return jnp.dot(a, b, preferred_element_type=jnp.float32)
-
-    both = product(jnp.concatenate([rows_high, rows_high], 1), jnp.concatenate([high, low], 0))
-    return both + product(rows_low, high)
+    return stacked(rows, values, 1, 0, SIX_TERMS)
 
 
 def rotate_kernel(turn, upper, lower, *outputs):
@@ -211,8 +194,7 @@
     for piece in pieces:
         stop = start + piece.shape[1]
         for index, output in enumerate(outputs):
-            rows = turn[width * index:width * (index + 1), :]
-            output[:, start:stop] = three_pass(rows, piece[...], ((1,), (0,)))
+            output[:, start:stop] = turned(turn[width * index:width * (index + 1), :], piece[...])
         start = stop
 
 

time: 92.1 us -> 94.1 us (1.022)
  Pallas kernels: 35.1 us -> 38.5 us
  waiting for transfers between devices: 48.1 us -> 46.8 us
    pallas_call x10, Pallas kernels: 3.37 us -> 5.38 us  [rotate(): pl.pallas_call(rotate_kernel, out_shape=(jax.ShapeDtypeStruct(upper.shape...]
    ppermute x15, waiting for transfers between devices: 48.1 us -> 46.8 us  [shifted(): lax.ppermute(block, axis, [((i - distance) % size, i) for i in range(size)])]
    pallas_call x7, Pallas kernels: 29.9 us -> 31 us  [square_call(): pl.pallas_call(kernel, out_shape=jax.ShapeDtypeStruct((size, size), opera...]
  transfers between devices with their start and end apart: 16 -> 16, of which waited for: 7 -> 7; matrix products, arithmetic and copies ran while one was open for 0% -> 0% of each run, Pallas kernels for 35% -> 36%
where the time goes in v6:
time: 94.1 us; the launch traced here: 94 us
  waiting for transfers between devices  46.8 us (50%)
  Pallas kernels  38.5 us (41%)
  starting transfers between devices  6.8 us (7%)
  local copies, waits for them, and re-layouts  0.98 us (1%)
    ppermute x15, waiting for transfers between devices, shifted(): lax.ppermute(block, axis, [((i - distance) % size, i) for i in range(size)])  46.8 us
    pallas_call x7, Pallas kernels, square_call(): pl.pallas_call(kernel, out_shape=jax.ShapeDtypeStruct((size, size), opera...  31 us
    ppermute x15, starting transfers between devices, shifted(): lax.ppermute(block, axis, [((i - distance) % size, i) for i in range(size)])  6.79 us
    pallas_call x10, Pallas kernels, rotate(): pl.pallas_call(rotate_kernel, out_shape=(jax.ShapeDtypeStruct(upper.shape...  5.38 us
  transfers between devices with their start and end apart: 16, of which 7 were waited for; matrix products, arithmetic and copies ran while one was open for 0% of the time, Pallas kernels for 36%

profile of v6, /device:TPU:0, one launch (start us, length us, event | category | flops | bytes accessed | tf_op | source)
XLA Modules:
  0.0 94.0 jit_solution(8064335153210704860)
XLA Ops:
  0.6 3.0 %collective-permute-start.3 = (f32[128,640]{1,0:T(8,128)}, f32[128,640]{1,0:T(8,128)S(1)}, u32[]{:S(2)}, u32[]{:S(2)}) collective-permute-start(f32[128,640]{1,0:T(8,128)} %refs_0_.1), channel_id=1, source_target_pairs={{1,0},{0,1},{3,2},{2,3},{5,4},{4,5},{7,6},{6,7},{9,8},{8,9},{11,10... | collective-permute-start | bytes 983048 | tf_op jit(solution)/shard_map/ppermute | solution.py:21
  3.7 1.6 %collective-permute-start.5 = (f32[128,640]{1,0:T(8,128)}, f32[128,640]{1,0:T(8,128)S(1)}, u32[]{:S(2)}, u32[]{:S(2)}) collective-permute-start(f32[128,640]{1,0:T(8,128)} %refs_0_.1), channel_id=1, source_target_pairs={{30,0},{0,2},{2,4},{4,6},{6,8},{8,10},{10,12},{12,14},{14,16},{16,... | collective-permute-start | bytes 983048 | tf_op jit(solution)/shard_map/ppermute | solution.py:21
  5.3 1.0 %copy-done = f32[128,640]{1,0:T(8,128)S(1)} copy-done((f32[128,640]{1,0:T(8,128)S(1)}, f32[128,640]{1,0:T(8,128)}, u32[]{:S(2)}) %copy-start) | copy-done | bytes 327704
  6.6 1.6 %collective-permute-start.2 = (f32[128,128]{1,0:T(8,128)S(1)}, f32[128,128]{1,0:T(8,128)S(1)}, u32[]{:S(2)}, u32[]{:S(2)}) collective-permute-start(f32[128,128]{1,0:T(8,128)S(1)} %shard_map.41.refs_0_), channel_id=1, source_target_pairs={{1,0},{0,1},{3,2},{2,3},{5,4},{4,5},{7,6},{6,7},{9,8},{8,9},{11,10... | collective-permute-start | bytes 196616 | tf_op jit(solution)/shard_map/ppermute | solution.py:21
  8.2 11.9 %collective-permute-done.2.refs_1_ = f32[128,128]{1,0:T(8,128)S(1)} collective-permute-done((f32[128,128]{1,0:T(8,128)S(1)}, f32[128,128]{1,0:T(8,128)S(1)}, u32[]{:S(2)}, u32[]{:S(2)}) %collective-permute-start.2) | collective-permute-done | bytes 65568 | tf_op jit(solution)/shard_map/ppermute | solution.py:21
  20.0 4.7 %shard_map.42.turn = f32[128,128]{1,0:T(8,128)S(1)} custom-call(f32[128,128]{1,0:T(8,128)S(1)} %shard_map.41.refs_0_, f32[128,128]{1,0:T(8,128)S(1)} %collective-permute-done.2.refs_1_), custom_call_target="tpu_custom_call" | custom-call | tf_op jit(solution)/shard_map/pallas_call | solution.py:220
  25.3 5.8 %collective-permute-done.4.turn = f32[128,128]{1,0:T(8,128)S(1)} collective-permute-done((f32[128,128]{1,0:T(8,128)S(1)}, f32[128,128]{1,0:T(8,128)S(1)}, u32[]{:S(2)}, u32[]{:S(2)}) %collective-permute-start.4) | collective-permute-done | bytes 65568 | tf_op jit(solution)/shard_map/ppermute | solution.py:21
  31.1 0.9 shard_map.44
  32.0 61.2 %while.14 = (s32[]{:T(128)}, f32[64,1536]{1,0:T(8,128)S(1)}, f32[64,1536]{1,0:T(8,128)S(1)}, f32[64,1536]{1,0:T(8,128)S(1)}, s32[]{:T(128)}) while((s32[]{:T(128)}, f32[64,1536]{1,0:T(8,128)S(1)}, f32[64,1536]{1,0:T(8,128)S(1)}, f32[64,1536]{1,0:T(8,128)S(1)}, s32[]{:T(128)}) %tuple.20), condition=%wide.region_1.0_spmd, body=%wide.region_0.0_spmd.sunk | while | flops 2 | bytes 1835149 | solution.py:293
  32.1 5.2 %eval_jaxpr.3.turn = f32[128,128]{1,0:T(8,128)S(1)} custom-call(f32[64,1536]{1,0:T(8,128)S(1)} %get-tuple-element.76.stay.upper, f32[64,1536]{1,0:T(8,128)S(1)} %get-tuple-element.77.moving.lower), custom_call_target="tpu_custom_call" | custom-call | tf_op jit(solution)/shard_map/while/body/eval_jaxpr/pallas_call | solution.py:220
  37.9 5.8 %collective-permute-done.turn = f32[128,128]{1,0:T(8,128)S(1)} collective-permute-done((f32[128,128]{1,0:T(8,128)S(1)}, f32[128,128]{1,0:T(8,128)S(1)}, u32[]{:S(2)}, u32[]{:S(2)}) %collective-permute-start) | collective-permute-done | bytes 65568 | tf_op jit(solution)/shard_map/while/body/eval_jaxpr/ppermute | solution.py:21
  44.3 5.2 %eval_jaxpr.3.turn = f32[128,128]{1,0:T(8,128)S(1)} custom-call(f32[64,1536]{1,0:T(8,128)S(1)} %get-tuple-element.76.stay.upper, f32[64,1536]{1,0:T(8,128)S(1)} %get-tuple-element.77.moving.lower), custom_call_target="tpu_custom_call" | custom-call | tf_op jit(solution)/shard_map/while/body/eval_jaxpr/pallas_call | solution.py:220
  49.6 0.6 eval_jaxpr.4
  50.1 5.8 %collective-permute-done.turn = f32[128,128]{1,0:T(8,128)S(1)} collective-permute-done((f32[128,128]{1,0:T(8,128)S(1)}, f32[128,128]{1,0:T(8,128)S(1)}, u32[]{:S(2)}, u32[]{:S(2)}) %collective-permute-start) | collective-permute-done | bytes 65568 | tf_op jit(solution)/shard_map/while/body/eval_jaxpr/ppermute | solution.py:21
  56.6 5.2 %eval_jaxpr.3.turn = f32[128,128]{1,0:T(8,128)S(1)} custom-call(f32[64,1536]{1,0:T(8,128)S(1)} %get-tuple-element.76.stay.upper, f32[64,1536]{1,0:T(8,128)S(1)} %get-tuple-element.77.moving.lower), custom_call_target="tpu_custom_call" | custom-call | tf_op jit(solution)/shard_map/while/body/eval_jaxpr/pallas_call | solution.py:220
  61.8 0.6 eval_jaxpr.4
  62.4 5.8 %collective-permute-done.turn = f32[128,128]{1,0:T(8,128)S(1)} collective-permute-done((f32[128,128]{1,0:T(8,128)S(1)}, f32[128,128]{1,0:T(8,128)S(1)}, u32[]{:S(2)}, u32[]{:S(2)}) %collective-permute-start) | collective-permute-done | bytes 65568 | tf_op jit(solution)/shard_map/while/body/eval_jaxpr/ppermute | solution.py:21
  68.8 5.2 %eval_jaxpr.3.turn = f32[128,128]{1,0:T(8,128)S(1)} custom-call(f32[64,1536]{1,0:T(8,128)S(1)} %get-tuple-element.76.stay.upper, f32[64,1536]{1,0:T(8,128)S(1)} %get-tuple-element.77.moving.lower), custom_call_target="tpu_custom_call" | custom-call | tf_op jit(solution)/shard_map/while/body/eval_jaxpr/pallas_call | solution.py:220
  74.1 0.6 eval_jaxpr.4
  74.6 5.8 %collective-permute-done.turn = f32[128,128]{1,0:T(8,128)S(1)} collective-permute-done((f32[128,128]{1,0:T(8,128)S(1)}, f32[128,128]{1,0:T(8,128)S(1)}, u32[]{:S(2)}, u32[]{:S(2)}) %collective-permute-start) | collective-permute-done | bytes 65568 | tf_op jit(solution)/shard_map/while/body/eval_jaxpr/ppermute | solution.py:21
  81.0 5.2 %eval_jaxpr.3.turn = f32[128,128]{1,0:T(8,128)S(1)} custom-call(f32[64,1536]{1,0:T(8,128)S(1)} %get-tuple-element.76.stay.upper, f32[64,1536]{1,0:T(8,128)S(1)} %get-tuple-element.77.moving.lower), custom_call_target="tpu_custom_call" | custom-call | tf_op jit(solution)/shard_map/while/body/eval_jaxpr/pallas_call | solution.py:220
  86.3 0.6 eval_jaxpr.4
  86.9 5.8 %collective-permute-done.turn = f32[128,128]{1,0:T(8,128)S(1)} collective-permute-done((f32[128,128]{1,0:T(8,128)S(1)}, f32[128,128]{1,0:T(8,128)S(1)}, u32[]{:S(2)}, u32[]{:S(2)}) %collective-permute-start) | collective-permute-done | bytes 65568 | tf_op jit(solution)/shard_map/while/body/eval_jaxpr/ppermute | solution.py:21
  93.2 0.8 deliver.1
  (35 shorter events, 4.6 us)
Async XLA Ops:
  0.6 24.1 %collective-permute-start.3 = (f32[128,640]{1,0:T(8,128)}, f32[128,640]{1,0:T(8,128)S(1)}, u32[]{:S(2)}, u32[]{:S(2)}) collective-permute-start(f32[128,640]{1,0:T(8,128)} %refs_0_.1), channel_id=1, source_target_pairs={{1,0},{0,1},{3,2},{2,3},{5,4},{4,5},{7,6},{6,7},{9,8},{8,9},{11,10... | collective-permute-start | bytes 983048 | tf_op jit(solution)/shard_map/ppermute | solution.py:21
  3.7 27.4 %collective-permute-start.6 = (f32[128,640]{1,0:T(8,128)}, f32[128,640]{1,0:T(8,128)S(1)}, u32[]{:S(2)}, u32[]{:S(2)}) collective-permute-start(f32[128,640]{1,0:T(8,128)} %refs_0_.1), channel_id=1, source_target_pairs={{1,2},{0,3},{3,4},{2,5},{5,6},{4,7},{7,8},{6,9},{9,10},{8,11},{11,... | collective-permute-start | bytes 983048 | tf_op jit(solution)/shard_map/ppermute | solution.py:268
  3.7 27.4 %collective-permute-start.5 = (f32[128,640]{1,0:T(8,128)}, f32[128,640]{1,0:T(8,128)S(1)}, u32[]{:S(2)}, u32[]{:S(2)}) collective-permute-start(f32[128,640]{1,0:T(8,128)} %refs_0_.1), channel_id=1, source_target_pairs={{30,0},{0,2},{2,4},{4,6},{6,8},{8,10},{10,12},{12,14},{14,16},{16,... | collective-permute-start | bytes 983048 | tf_op jit(solution)/shard_map/ppermute | solution.py:21
  5.3 1.0 %copy-start = (f32[128,640]{1,0:T(8,128)S(1)}, f32[128,640]{1,0:T(8,128)}, u32[]{:S(2)}) copy-start(f32[128,640]{1,0:T(8,128)} %refs_0_.1) | copy-start | bytes 983044
  6.2 18.5 %copy-start.1 = (f32[128,640]{1,0:T(8,128)S(1)}, f32[128,640]{1,0:T(8,128)}, u32[]{:S(2)}) copy-start(f32[128,640]{1,0:T(8,128)} %refs_0_.1) | copy-start | bytes 983044
  6.6 18.2 %copy-start.2 = (f32[128,256]{1,0:T(8,128)S(1)}, f32[128,256]{1,0:T(8,128)}, u32[]{:S(2)}) copy-start(f32[128,256]{1,0:T(8,128)} %refs_2_.1) | copy-start | bytes 393220
  6.6 13.4 %collective-permute-start.2 = (f32[128,128]{1,0:T(8,128)S(1)}, f32[128,128]{1,0:T(8,128)S(1)}, u32[]{:S(2)}, u32[]{:S(2)}) collective-permute-start(f32[128,128]{1,0:T(8,128)S(1)} %shard_map.41.refs_0_), channel_id=1, source_target_pairs={{1,0},{0,1},{3,2},{2,3},{5,4},{4,5},{7,6},{6,7},{9,8},{8,9},{11,10... | collective-permute-start | bytes 196616 | tf_op jit(solution)/shard_map/ppermute | solution.py:21
  8.1 23.0 %collective-permute-start.7 = (f32[128,256]{1,0:T(8,128)}, f32[128,256]{1,0:T(8,128)S(1)}, u32[]{:S(2)}, u32[]{:S(2)}) collective-permute-start(f32[128,256]{1,0:T(8,128)} %refs_2_.1), channel_id=1, source_target_pairs={{30,0},{0,2},{2,4},{4,6},{6,8},{8,10},{10,12},{12,14},{14,16},{16,... | collective-permute-start | bytes 393224 | tf_op jit(solution)/shard_map/ppermute | solution.py:21
  24.7 6.4 %collective-permute-start.4 = (f32[128,128]{1,0:T(8,128)S(1)}, f32[128,128]{1,0:T(8,128)S(1)}, u32[]{:S(2)}, u32[]{:S(2)}) collective-permute-start(f32[128,128]{1,0:T(8,128)S(1)} %shard_map.42.turn), channel_id=1, source_target_pairs={{30,0},{0,2},{2,4},{4,6},{6,8},{8,10},{10,12},{12,14},{14,16},{16,... | collective-permute-start | bytes 196616 | tf_op jit(solution)/shard_map/ppermute | solution.py:21
  32.0 11.7 %collective-permute-start.1 = (f32[64,1536]{1,0:T(8,128)S(1)}, f32[64,1536]{1,0:T(8,128)S(1)}, u32[]{:S(2)}, u32[]{:S(2)}) collective-permute-start(f32[64,1536]{1,0:T(8,128)S(1)} %get-tuple-element.77.moving.lower), channel_id=1, source_target_pairs={{30,0},{0,2},{2,4},{4,6},{6,8},{8,10},{10,12},{12,14},{14,16},{16,... | collective-permute-start | bytes 1179656 | tf_op jit(solution)/shard_map/while/body/eval_jaxpr/ppermute | solution.py:21
  37.3 6.4 %collective-permute-start = (f32[128,128]{1,0:T(8,128)S(1)}, f32[128,128]{1,0:T(8,128)S(1)}, u32[]{:S(2)}, u32[]{:S(2)}) collective-permute-start(f32[128,128]{1,0:T(8,128)S(1)} %eval_jaxpr.3.turn), channel_id=1, source_target_pairs={{30,0},{0,2},{2,4},{4,6},{6,8},{8,10},{10,12},{12,14},{14,16},{16,... | collective-permute-start | bytes 196616 | tf_op jit(solution)/shard_map/while/body/eval_jaxpr/ppermute | solution.py:21
  44.3 11.7 %collective-permute-start.1 = (f32[64,1536]{1,0:T(8,128)S(1)}, f32[64,1536]{1,0:T(8,128)S(1)}, u32[]{:S(2)}, u32[]{:S(2)}) collective-permute-start(f32[64,1536]{1,0:T(8,128)S(1)} %get-tuple-element.77.moving.lower), channel_id=1, source_target_pairs={{30,0},{0,2},{2,4},{4,6},{6,8},{8,10},{10,12},{12,14},{14,16},{16,... | collective-permute-start | bytes 1179656 | tf_op jit(solution)/shard_map/while/body/eval_jaxpr/ppermute | solution.py:21
  49.5 6.4 %collective-permute-start = (f32[128,128]{1,0:T(8,128)S(1)}, f32[128,128]{1,0:T(8,128)S(1)}, u32[]{:S(2)}, u32[]{:S(2)}) collective-permute-start(f32[128,128]{1,0:T(8,128)S(1)} %eval_jaxpr.3.turn), channel_id=1, source_target_pairs={{30,0},{0,2},{2,4},{4,6},{6,8},{8,10},{10,12},{12,14},{14,16},{16,... | collective-permute-start | bytes 196616 | tf_op jit(solution)/shard_map/while/body/eval_jaxpr/ppermute | solution.py:21
  56.5 11.7 %collective-permute-start.1 = (f32[64,1536]{1,0:T(8,128)S(1)}, f32[64,1536]{1,0:T(8,128)S(1)}, u32[]{:S(2)}, u32[]{:S(2)}) collective-permute-start(f32[64,1536]{1,0:T(8,128)S(1)} %get-tuple-element.77.moving.lower), channel_id=1, source_target_pairs={{30,0},{0,2},{2,4},{4,6},{6,8},{8,10},{10,12},{12,14},{14,16},{16,... | collective-permute-start | bytes 1179656 | tf_op jit(solution)/shard_map/while/body/eval_jaxpr/ppermute | solution.py:21
  61.8 6.4 %collective-permute-start = (f32[128,128]{1,0:T(8,128)S(1)}, f32[128,128]{1,0:T(8,128)S(1)}, u32[]{:S(2)}, u32[]{:S(2)}) collective-permute-start(f32[128,128]{1,0:T(8,128)S(1)} %eval_jaxpr.3.turn), channel_id=1, source_target_pairs={{30,0},{0,2},{2,4},{4,6},{6,8},{8,10},{10,12},{12,14},{14,16},{16,... | collective-permute-start | bytes 196616 | tf_op jit(solution)/shard_map/while/body/eval_jaxpr/ppermute | solution.py:21
  68.7 11.7 %collective-permute-start.1 = (f32[64,1536]{1,0:T(8,128)S(1)}, f32[64,1536]{1,0:T(8,128)S(1)}, u32[]{:S(2)}, u32[]{:S(2)}) collective-permute-start(f32[64,1536]{1,0:T(8,128)S(1)} %get-tuple-element.77.moving.lower), channel_id=1, source_target_pairs={{30,0},{0,2},{2,4},{4,6},{6,8},{8,10},{10,12},{12,14},{14,16},{16,... | collective-permute-start | bytes 1179656 | tf_op jit(solution)/shard_map/while/body/eval_jaxpr/ppermute | solution.py:21
  74.0 6.4 %collective-permute-start = (f32[128,128]{1,0:T(8,128)S(1)}, f32[128,128]{1,0:T(8,128)S(1)}, u32[]{:S(2)}, u32[]{:S(2)}) collective-permute-start(f32[128,128]{1,0:T(8,128)S(1)} %eval_jaxpr.3.turn), channel_id=1, source_target_pairs={{30,0},{0,2},{2,4},{4,6},{6,8},{8,10},{10,12},{12,14},{14,16},{16,... | collective-permute-start | bytes 196616 | tf_op jit(solution)/shard_map/while/body/eval_jaxpr/ppermute | solution.py:21
  81.0 11.7 %collective-permute-start.1 = (f32[64,1536]{1,0:T(8,128)S(1)}, f32[64,1536]{1,0:T(8,128)S(1)}, u32[]{:S(2)}, u32[]{:S(2)}) collective-permute-start(f32[64,1536]{1,0:T(8,128)S(1)} %get-tuple-element.77.moving.lower), channel_id=1, source_target_pairs={{30,0},{0,2},{2,4},{4,6},{6,8},{8,10},{10,12},{12,14},{14,16},{16,... | collective-permute-start | bytes 1179656 | tf_op jit(solution)/shard_map/while/body/eval_jaxpr/ppermute | solution.py:21
  86.2 6.4 %collective-permute-start = (f32[128,128]{1,0:T(8,128)S(1)}, f32[128,128]{1,0:T(8,128)S(1)}, u32[]{:S(2)}, u32[]{:S(2)}) collective-permute-start(f32[128,128]{1,0:T(8,128)S(1)} %eval_jaxpr.3.turn), channel_id=1, source_target_pairs={{30,0},{0,2},{2,4},{4,6},{6,8},{8,10},{10,12},{12,14},{14,16},{16,... | collective-permute-start | bytes 196616 | tf_op jit(solution)/shard_map/while/body/eval_jaxpr/ppermute | solution.py:21
